TPU v7x, 256 devices: a whole 4x4x8 slice. The times are simulated.
256 devices in a mesh: grp: 32 (over z, y), mem: 8 (over x, core).
Axes of the slice: x: 4, y: 4, z: 8, core: 2. Of those that a mesh axis runs over, the one named last changes fastest.
Arguments:
- potential: float32 [512, 512, 512], P(('grp', 'mem')), may hold values from -6 to 6
- source: float32 [512, 512, 512], P(('grp', 'mem')), may hold values from -20 to 20
- side_faces: float32 [256, 4, 256], P(('grp', 'mem')), may hold values from -6 to 6
- end_faces: float32 [2, 256, 256], replicated, may hold values from -6 to 6
Outputs:
- corrected: float32 [512, 512, 512], P(('grp', 'mem'))
- correction: float32 [256, 256, 256], P(('grp', 'mem'))
All inputs are finite; a program needn't handle non-finite values.
Results may differ from a plain program's by a relative error of at most 0.00002.
Values sent between devices are 32-bit elements; how exact they have to be, the bound alone decides.
A program may use at most 64 MiB of HBM per device.

v0:
```python
import jax
import jax.numpy as jnp
from jax import lax
from jax.sharding import PartitionSpec as P

SWEEPS = 8


def padded_2(shard, sides, width):
    edges = {}
    for axis, dim in sides:
        count, length = (lax.axis_size(axis), shard.shape[dim])
        up = [(i, (i + 1) % count) for i in range(count - 1)]
        last = lax.slice_in_dim(shard, length - width, length, axis=dim)
        initial = lax.slice_in_dim(shard, 0, width, axis=dim)
        edges[dim] = (
            lax.ppermute(last, axis, up),
            lax.ppermute(initial, axis, [(b, a) for a, b in up]),
        )
    done = []
    for _, dim in sides:
        low, high = edges[dim]
        around = [(width, width) if d in done else (0, 0) for d in range(shard.ndim)]
        shard = jnp.concatenate([jnp.pad(low, around), shard, jnp.pad(high, around)], axis=dim)
        done.append(dim)
    return shard


def from_behind(value, axis, steps):
    count = lax.axis_size(axis)
    initial, last = (max(0, -steps), min(count, count - steps))
    return lax.ppermute(value, axis, [(source, source + steps) for source in range(initial, last)])


def fine_operator(padded):
    center = padded[1:-1, 1:-1, 1:-1]
    beside = padded[2:, 1:-1, 1:-1] + padded[:-2, 1:-1, 1:-1]
    beside = beside + padded[1:-1, 2:, 1:-1] + padded[1:-1, :-2, 1:-1]
    beside = beside + padded[1:-1, 1:-1, 2:] + padded[1:-1, 1:-1, :-2]
    return 4.0 * (6.0 * center - beside)


def restrict_axis(values, direction, before):
    even_part = lax.slice_in_dim(values, 0, None, 2, direction)
    odd_part = lax.slice_in_dim(values, 1, None, 2, direction)
    length = odd_part.shape[direction]
    earlier = jnp.concatenate(
        [before, lax.slice_in_dim(odd_part, 0, length - 1, 1, direction)], direction
    )
    return 0.5 * even_part + 0.25 * (odd_part + earlier)


def zero_slice(values, direction):
    return jnp.zeros_like(lax.slice_in_dim(values, 0, 1, 1, direction))


def prolong_axis(values, direction, beyond):
    length = values.shape[direction]
    following = jnp.concatenate(
        [lax.slice_in_dim(values, 1, length, 1, direction), beyond], direction
    )
    middle = 0.5 * (values + following)
    paired = jnp.stack([values, middle], direction + 1)
    new_shape = list(values.shape)
    new_shape[direction] = 2 * length
    return paired.reshape(new_shape)


def last_slice(values, direction):
    length = values.shape[direction]
    return lax.slice_in_dim(values, length - 1, length, 1, direction)


def side_sum(values, side_faces):
    front_face = side_faces[:, 0:1, :]
    back_face = side_faces[:, 1:2, :]
    left_face = side_faces[:, 2, :][:, :, None]
    right_face = side_faces[:, 3, :][:, :, None]
    front_cells = jnp.concatenate([front_face, values[:, :-1, :]], 1)
    back_cells = jnp.concatenate([values[:, 1:, :], back_face], 1)
    left_cells = jnp.concatenate([left_face, values[:, :, :-1]], 2)
    right_cells = jnp.concatenate([values[:, :, 1:], right_face], 2)
    return front_cells + back_cells + (left_cells + right_cells)


def smooth_red_black(
    forcing, side_faces, end_faces, offset, at_first, at_last, neighbour_fn, initial
):
    planes = forcing.shape[0]
    depth_ids = offset + lax.broadcasted_iota(jnp.int32, forcing.shape, 0)
    row_ids = lax.broadcasted_iota(jnp.int32, forcing.shape, 1)
    col_ids = lax.broadcasted_iota(jnp.int32, forcing.shape, 2)
    parity = (depth_ids + row_ids + col_ids) % 2

    def one_sweep(counter, values):
        for colour in (0, 1):
            padded = neighbour_fn(values)
            lower_face = jnp.where(at_first, end_faces[0], padded[0])
            upper_face = jnp.where(at_last, end_faces[1], padded[-1])
            under_plane = jnp.concatenate([lower_face[None], padded[1:planes]], 0)
            over_plane = jnp.concatenate([padded[2 : planes + 1], upper_face[None]], 0)
            neighbours = under_plane + over_plane + side_sum(values, side_faces)
            update = jnp.logical_and(parity == colour, True)
            values = jnp.where(update, (forcing + neighbours) / 6.0, values)
        return values

    return lax.fori_loop(0, SWEEPS, one_sweep, initial)


def per_device(potential, source, side_faces, end_faces):
    groups = lax.axis_size("grp")
    members = lax.axis_size("mem")
    devices = groups * members
    position = lax.axis_index("grp") * members + lax.axis_index("mem")
    haloed = padded_2(potential, ((("grp", "mem"), 0),), 1)
    padded = jnp.pad(haloed, ((0, 0), (1, 1), (1, 1)))
    residual = source - fine_operator(padded)
    before = from_behind(residual[-1:], ("grp", "mem"), 1)
    forcing = restrict_axis(residual, 0, before)
    for direction in (1, 2):
        forcing = restrict_axis(forcing, direction, zero_slice(forcing, direction))
    planes = forcing.shape[0]

    def plane_neighbours(values):
        return padded_2(values, ((("grp", "mem"), 0),), 1)

    correction = smooth_red_black(
        forcing,
        side_faces,
        end_faces,
        position * planes,
        position == 0,
        position == devices - 1,
        plane_neighbours,
        jnp.zeros_like(forcing),
    )
    upper_plane = from_behind(correction, ("grp", "mem"), -1)
    beyond = jnp.where(position == devices - 1, correction, upper_plane)
    refined = prolong_axis(correction, 0, beyond)
    for direction in (1, 2):
        refined = prolong_axis(refined, direction, last_slice(refined, direction))
    return (potential + refined, correction)


def solution(mesh):
    placed = (
        P(("grp", "mem"), None, None),
        P(("grp", "mem"), None, None),
        P(("grp", "mem"), None, None),
        P(),
    )
    return jax.shard_map(
        per_device,
        mesh=mesh,
        in_specs=placed,
        out_specs=(P(("grp", "mem"), None, None), P(("grp", "mem"), None, None)),
        check_vma=False,
    )
```

profile of v0, /device:TPU:129, one launch (start us, length us, event | category | flops | bytes accessed | tf_op | source)
XLA Modules:
  0.0 379.3 jit_solution(4192511227677884742)
XLA Ops:
  5.1 3.1 collective-permute-start.5
  8.3 10.4 %collective-permute-done.4 = f32[1,512,512]{2,1,0:T(8,128)S(1)} collective-permute-done((f32[1,512,512]{2,1,0:T(8,128)S(1)}, f32[1,512,512]{2,1,0:T(8,128)S(1)}, u32[]{:S(2)}, u32[]{:S(2)}) %collective-permute-start.4) | collective-permute-done | bytes 1048608 | tf_op jit(solution)/shard_map/ppermute | solution.py:18
  24.8 4.4 %collective-permute-start.6 = (f32[1,512,512]{2,1,0:T(8,128)S(1)}, f32[1,512,512]{2,1,0:T(8,128)}, u32[]{:S(2)}, u32[]{:S(2)}) collective-permute-start(f32[1,512,512]{2,1,0:T(8,128)S(1)} %slice.164), channel_id=1, source_target_pairs={{0,1},{1,2},{2,3},{3,4},{4,5},{5,6},{6,7},{7,8},{8,9},{9,10},{10,1... | collective-permute-start | bytes 3145736 | tf_op jit(solution)/shard_map/ppermute | solution.py:32
  29.3 11.7 %collective-permute-done.6 = f32[1,512,512]{2,1,0:T(8,128)} collective-permute-done((f32[1,512,512]{2,1,0:T(8,128)S(1)}, f32[1,512,512]{2,1,0:T(8,128)}, u32[]{:S(2)}, u32[]{:S(2)}) %collective-permute-start.6) | collective-permute-done | bytes 1048608 | tf_op jit(solution)/shard_map/ppermute | solution.py:32
  41.0 3.2 fusion.27
  47.1 3.7 slice.127
  52.9 12.5 %slice.131 = f32[1,256,256]{2,1,0:T(8,128)S(1)} slice(f32[1,256,512]{2,1,0:T(8,128)} %multiply_add_fusion), slice={[0:1:1], [0:256:1], [1:512:2]} | slice | bytes 524288 | tf_op jit(solution)/shard_map/slice | solution.py:45
  65.4 13.0 %slice.130 = f32[1,256,256]{2,1,0:T(8,128)} slice(f32[1,256,512]{2,1,0:T(8,128)} %multiply_add_fusion), slice={[0:1:1], [0:256:1], [0:512:2]} | slice | bytes 524288 | tf_op jit(solution)/shard_map/slice | solution.py:44
  79.5 266.2 %while.11 = (s32[]{:T(128)}, f32[1,256,256]{2,1,0:T(8,128)S(1)}, pred[]{:T(512)}, f32[2,256,256]{2,1,0:T(8,128)S(1)}, pred[]{:T(512)}, /*index=5*/f32[1,4,256]{2...) while((s32[]{:T(128)}, f32[1,256,256]{2,1,0:T(8,128)S(1)}, ...), condition=%wide.region_1.2_spmd.clone, body=%wide.region_0.1_spmd.clone.sunk | while | flops 3670019 | bytes 14682416 | solution.py:107
  79.5 18.4 %collective-permute-start = (f32[1,256,256]{2,1,0:T(8,128)S(1)}, f32[1,256,256]{2,1,0:T(8,128)}, u32[]{:S(2)}, u32[]{:S(2)}) collective-permute-start(f32[1,256,256]{2,1,0:T(8,128)S(1)} %broadcast_select_fusion.2), channel_id=1, source_target_pairs={{1,0},{2,1},{3,2},{4,3},{5,4},{6,5},{7,6},{8,7},{9,8},{10,9},{11,1... | collective-permute-start | bytes 786440 | tf_op jit(solution)/shard_map/while/body/eval_jaxpr/ppermute | solution.py:18
  105.5 9.2 %collective-permute-start.2 = (f32[1,256,256]{2,1,0:T(8,128)S(1)}, f32[1,256,256]{2,1,0:T(8,128)S(1)}, u32[]{:S(2)}, u32[]{:S(2)}) collective-permute-start(f32[1,256,256]{2,1,0:T(8,128)S(1)} %fusion.50), channel_id=1, source_target_pairs={{1,0},{2,1},{3,2},{4,3},{5,4},{6,5},{7,6},{8,7},{9,8},{10,9},{11,1... | collective-permute-start | bytes 786440 | tf_op jit(solution)/shard_map/while/body/eval_jaxpr/ppermute | solution.py:18
  120.3 9.8 %collective-permute-start = (f32[1,256,256]{2,1,0:T(8,128)S(1)}, f32[1,256,256]{2,1,0:T(8,128)}, u32[]{:S(2)}, u32[]{:S(2)}) collective-permute-start(f32[1,256,256]{2,1,0:T(8,128)S(1)} %broadcast_select_fusion.2), channel_id=1, source_target_pairs={{1,0},{2,1},{3,2},{4,3},{5,4},{6,5},{7,6},{8,7},{9,8},{10,9},{11,1... | collective-permute-start | bytes 786440 | tf_op jit(solution)/shard_map/while/body/eval_jaxpr/ppermute | solution.py:18
  137.7 9.2 %collective-permute-start.2 = (f32[1,256,256]{2,1,0:T(8,128)S(1)}, f32[1,256,256]{2,1,0:T(8,128)S(1)}, u32[]{:S(2)}, u32[]{:S(2)}) collective-permute-start(f32[1,256,256]{2,1,0:T(8,128)S(1)} %fusion.50), channel_id=1, source_target_pairs={{1,0},{2,1},{3,2},{4,3},{5,4},{6,5},{7,6},{8,7},{9,8},{10,9},{11,1... | collective-permute-start | bytes 786440 | tf_op jit(solution)/shard_map/while/body/eval_jaxpr/ppermute | solution.py:18
  149.1 3.1 collective-permute-done.3
  152.5 9.8 %collective-permute-start = (f32[1,256,256]{2,1,0:T(8,128)S(1)}, f32[1,256,256]{2,1,0:T(8,128)}, u32[]{:S(2)}, u32[]{:S(2)}) collective-permute-start(f32[1,256,256]{2,1,0:T(8,128)S(1)} %broadcast_select_fusion.2), channel_id=1, source_target_pairs={{1,0},{2,1},{3,2},{4,3},{5,4},{6,5},{7,6},{8,7},{9,8},{10,9},{11,1... | collective-permute-start | bytes 786440 | tf_op jit(solution)/shard_map/while/body/eval_jaxpr/ppermute | solution.py:18
  169.9 9.2 %collective-permute-start.2 = (f32[1,256,256]{2,1,0:T(8,128)S(1)}, f32[1,256,256]{2,1,0:T(8,128)S(1)}, u32[]{:S(2)}, u32[]{:S(2)}) collective-permute-start(f32[1,256,256]{2,1,0:T(8,128)S(1)} %fusion.50), channel_id=1, source_target_pairs={{1,0},{2,1},{3,2},{4,3},{5,4},{6,5},{7,6},{8,7},{9,8},{10,9},{11,1... | collective-permute-start | bytes 786440 | tf_op jit(solution)/shard_map/while/body/eval_jaxpr/ppermute | solution.py:18
  184.7 9.8 %collective-permute-start = (f32[1,256,256]{2,1,0:T(8,128)S(1)}, f32[1,256,256]{2,1,0:T(8,128)}, u32[]{:S(2)}, u32[]{:S(2)}) collective-permute-start(f32[1,256,256]{2,1,0:T(8,128)S(1)} %broadcast_select_fusion.2), channel_id=1, source_target_pairs={{1,0},{2,1},{3,2},{4,3},{5,4},{6,5},{7,6},{8,7},{9,8},{10,9},{11,1... | collective-permute-start | bytes 786440 | tf_op jit(solution)/shard_map/while/body/eval_jaxpr/ppermute | solution.py:18
  202.1 9.2 %collective-permute-start.2 = (f32[1,256,256]{2,1,0:T(8,128)S(1)}, f32[1,256,256]{2,1,0:T(8,128)S(1)}, u32[]{:S(2)}, u32[]{:S(2)}) collective-permute-start(f32[1,256,256]{2,1,0:T(8,128)S(1)} %fusion.50), channel_id=1, source_target_pairs={{1,0},{2,1},{3,2},{4,3},{5,4},{6,5},{7,6},{8,7},{9,8},{10,9},{11,1... | collective-permute-start | bytes 786440 | tf_op jit(solution)/shard_map/while/body/eval_jaxpr/ppermute | solution.py:18
  216.9 9.8 %collective-permute-start = (f32[1,256,256]{2,1,0:T(8,128)S(1)}, f32[1,256,256]{2,1,0:T(8,128)}, u32[]{:S(2)}, u32[]{:S(2)}) collective-permute-start(f32[1,256,256]{2,1,0:T(8,128)S(1)} %broadcast_select_fusion.2), channel_id=1, source_target_pairs={{1,0},{2,1},{3,2},{4,3},{5,4},{6,5},{7,6},{8,7},{9,8},{10,9},{11,1... | collective-permute-start | bytes 786440 | tf_op jit(solution)/shard_map/while/body/eval_jaxpr/ppermute | solution.py:18
  234.3 9.2 %collective-permute-start.2 = (f32[1,256,256]{2,1,0:T(8,128)S(1)}, f32[1,256,256]{2,1,0:T(8,128)S(1)}, u32[]{:S(2)}, u32[]{:S(2)}) collective-permute-start(f32[1,256,256]{2,1,0:T(8,128)S(1)} %fusion.50), channel_id=1, source_target_pairs={{1,0},{2,1},{3,2},{4,3},{5,4},{6,5},{7,6},{8,7},{9,8},{10,9},{11,1... | collective-permute-start | bytes 786440 | tf_op jit(solution)/shard_map/while/body/eval_jaxpr/ppermute | solution.py:18
  245.7 3.1 collective-permute-done.3
  249.1 9.8 %collective-permute-start = (f32[1,256,256]{2,1,0:T(8,128)S(1)}, f32[1,256,256]{2,1,0:T(8,128)}, u32[]{:S(2)}, u32[]{:S(2)}) collective-permute-start(f32[1,256,256]{2,1,0:T(8,128)S(1)} %broadcast_select_fusion.2), channel_id=1, source_target_pairs={{1,0},{2,1},{3,2},{4,3},{5,4},{6,5},{7,6},{8,7},{9,8},{10,9},{11,1... | collective-permute-start | bytes 786440 | tf_op jit(solution)/shard_map/while/body/eval_jaxpr/ppermute | solution.py:18
  266.5 9.2 %collective-permute-start.2 = (f32[1,256,256]{2,1,0:T(8,128)S(1)}, f32[1,256,256]{2,1,0:T(8,128)S(1)}, u32[]{:S(2)}, u32[]{:S(2)}) collective-permute-start(f32[1,256,256]{2,1,0:T(8,128)S(1)} %fusion.50), channel_id=1, source_target_pairs={{1,0},{2,1},{3,2},{4,3},{5,4},{6,5},{7,6},{8,7},{9,8},{10,9},{11,1... | collective-permute-start | bytes 786440 | tf_op jit(solution)/shard_map/while/body/eval_jaxpr/ppermute | solution.py:18
  281.3 9.8 %collective-permute-start = (f32[1,256,256]{2,1,0:T(8,128)S(1)}, f32[1,256,256]{2,1,0:T(8,128)}, u32[]{:S(2)}, u32[]{:S(2)}) collective-permute-start(f32[1,256,256]{2,1,0:T(8,128)S(1)} %broadcast_select_fusion.2), channel_id=1, source_target_pairs={{1,0},{2,1},{3,2},{4,3},{5,4},{6,5},{7,6},{8,7},{9,8},{10,9},{11,1... | collective-permute-start | bytes 786440 | tf_op jit(solution)/shard_map/while/body/eval_jaxpr/ppermute | solution.py:18
  298.7 9.2 %collective-permute-start.2 = (f32[1,256,256]{2,1,0:T(8,128)S(1)}, f32[1,256,256]{2,1,0:T(8,128)S(1)}, u32[]{:S(2)}, u32[]{:S(2)}) collective-permute-start(f32[1,256,256]{2,1,0:T(8,128)S(1)} %fusion.50), channel_id=1, source_target_pairs={{1,0},{2,1},{3,2},{4,3},{5,4},{6,5},{7,6},{8,7},{9,8},{10,9},{11,1... | collective-permute-start | bytes 786440 | tf_op jit(solution)/shard_map/while/body/eval_jaxpr/ppermute | solution.py:18
  313.5 9.8 %collective-permute-start = (f32[1,256,256]{2,1,0:T(8,128)S(1)}, f32[1,256,256]{2,1,0:T(8,128)}, u32[]{:S(2)}, u32[]{:S(2)}) collective-permute-start(f32[1,256,256]{2,1,0:T(8,128)S(1)} %broadcast_select_fusion.2), channel_id=1, source_target_pairs={{1,0},{2,1},{3,2},{4,3},{5,4},{6,5},{7,6},{8,7},{9,8},{10,9},{11,1... | collective-permute-start | bytes 786440 | tf_op jit(solution)/shard_map/while/body/eval_jaxpr/ppermute | solution.py:18
  330.9 9.2 %collective-permute-start.2 = (f32[1,256,256]{2,1,0:T(8,128)S(1)}, f32[1,256,256]{2,1,0:T(8,128)S(1)}, u32[]{:S(2)}, u32[]{:S(2)}) collective-permute-start(f32[1,256,256]{2,1,0:T(8,128)S(1)} %fusion.50), channel_id=1, source_target_pairs={{1,0},{2,1},{3,2},{4,3},{5,4},{6,5},{7,6},{8,7},{9,8},{10,9},{11,1... | collective-permute-start | bytes 786440 | tf_op jit(solution)/shard_map/while/body/eval_jaxpr/ppermute | solution.py:18
  342.3 3.1 collective-permute-done.3
  345.7 10.0 %collective-permute-start.7 = (f32[1,256,256]{2,1,0:T(8,128)S(1)}, f32[1,256,256]{2,1,0:T(8,128)S(1)}, u32[]{:S(2)}, u32[]{:S(2)}) collective-permute-start(f32[1,256,256]{2,1,0:T(8,128)S(1)} %get-tuple-element.76), channel_id=1, source_target_pairs={{1,0},{2,1},{3,2},{4,3},{5,4},{6,5},{7,6},{8,7},{9,8},{10,9},{11,1... | collective-permute-start | bytes 786440 | tf_op jit(solution)/shard_map/ppermute | solution.py:32
  364.9 6.3 %copy.17 = f32[2,512,256,2]{1,0,3,2:T(2,128)} copy(f32[2,512,256,2]{2,0,1,3:T(2,128)} %pad_maximum_fusion.10) | data formatting | bytes 4194304 | tf_op jit(solution)/shard_map/stack | solution.py:63
  371.2 4.0 %bitcast_add_fusion = f32[2,512,512]{1,0,2:T(2,128)} fusion(f32[2,512,512]{1,0,2:T(2,128)S(1)} %copy-done.5, f32[2,512,256,2]{1,0,3,2:T(2,128)} %copy.17), kind=kLoop, calls=%fused_computation.53 | loop fusion | flops 524288 | bytes 6291456 | tf_op jit(solution)/shard_map/add | solution.py:142
  375.1 4.1 %copy.19 = f32[2,512,512]{2,1,0:T(8,128)} copy(f32[2,512,512]{1,0,2:T(2,128)} %bitcast_add_fusion) | data formatting | bytes 4194304
  (179 shorter events, 120.8 us)
Async XLA Ops:
  2.5 16.2 %collective-permute-start.4 = (f32[1,512,512]{2,1,0:T(8,128)S(1)}, f32[1,512,512]{2,1,0:T(8,128)S(1)}, u32[]{:S(2)}, u32[]{:S(2)}) collective-permute-start(f32[1,512,512]{2,1,0:T(8,128)S(1)} %get-tuple-element.106), channel_id=1, source_target_pairs={{1,0},{2,1},{3,2},{4,3},{5,4},{6,5},{7,6},{8,7},{9,8},{10,9},{11,1... | collective-permute-start | bytes 3145736 | tf_op jit(solution)/shard_map/ppermute | solution.py:18
  5.1 14.9 %collective-permute-start.5 = (f32[1,512,512]{2,1,0:T(8,128)S(1)}, f32[1,512,512]{2,1,0:T(8,128)S(1)}, u32[]{:S(2)}, u32[]{:S(2)}) collective-permute-start(f32[1,512,512]{2,1,0:T(8,128)S(1)} %get-tuple-element.105), channel_id=1, source_target_pairs={{0,1},{1,2},{2,3},{3,4},{4,5},{5,6},{6,7},{7,8},{8,9},{9,10},{10,1... | collective-permute-start | bytes 3145736 | tf_op jit(solution)/shard_map/ppermute | solution.py:17
  24.8 16.1 %collective-permute-start.6 = (f32[1,512,512]{2,1,0:T(8,128)S(1)}, f32[1,512,512]{2,1,0:T(8,128)}, u32[]{:S(2)}, u32[]{:S(2)}) collective-permute-start(f32[1,512,512]{2,1,0:T(8,128)S(1)} %slice.164), channel_id=1, source_target_pairs={{0,1},{1,2},{2,3},{3,4},{4,5},{5,6},{6,7},{7,8},{8,9},{9,10},{10,1... | collective-permute-start | bytes 3145736 | tf_op jit(solution)/shard_map/ppermute | solution.py:32
  79.5 24.4 %collective-permute-start = (f32[1,256,256]{2,1,0:T(8,128)S(1)}, f32[1,256,256]{2,1,0:T(8,128)}, u32[]{:S(2)}, u32[]{:S(2)}) collective-permute-start(f32[1,256,256]{2,1,0:T(8,128)S(1)} %broadcast_select_fusion.2), channel_id=1, source_target_pairs={{1,0},{2,1},{3,2},{4,3},{5,4},{6,5},{7,6},{8,7},{9,8},{10,9},{11,1... | collective-permute-start | bytes 786440 | tf_op jit(solution)/shard_map/while/body/eval_jaxpr/ppermute | solution.py:18
  98.0 5.9 %collective-permute-start.1 = (f32[1,256,256]{2,1,0:T(8,128)S(1)}, f32[1,256,256]{2,1,0:T(8,128)}, u32[]{:S(2)}, u32[]{:S(2)}) collective-permute-start(f32[1,256,256]{2,1,0:T(8,128)S(1)} %broadcast_select_fusion.2), channel_id=1, source_target_pairs={{0,1},{1,2},{2,3},{3,4},{4,5},{5,6},{6,7},{7,8},{8,9},{9,10},{10,1... | collective-permute-start | bytes 786440 | tf_op jit(solution)/shard_map/while/body/eval_jaxpr/ppermute | solution.py:17
  105.5 11.3 %collective-permute-start.2 = (f32[1,256,256]{2,1,0:T(8,128)S(1)}, f32[1,256,256]{2,1,0:T(8,128)S(1)}, u32[]{:S(2)}, u32[]{:S(2)}) collective-permute-start(f32[1,256,256]{2,1,0:T(8,128)S(1)} %fusion.50), channel_id=1, source_target_pairs={{1,0},{2,1},{3,2},{4,3},{5,4},{6,5},{7,6},{8,7},{9,8},{10,9},{11,1... | collective-permute-start | bytes 786440 | tf_op jit(solution)/shard_map/while/body/eval_jaxpr/ppermute | solution.py:18
  114.7 5.2 %collective-permute-start.3 = (f32[1,256,256]{2,1,0:T(8,128)S(1)}, f32[1,256,256]{2,1,0:T(8,128)S(1)}, u32[]{:S(2)}, u32[]{:S(2)}) collective-permute-start(f32[1,256,256]{2,1,0:T(8,128)S(1)} %fusion.50), channel_id=1, source_target_pairs={{0,1},{1,2},{2,3},{3,4},{4,5},{5,6},{6,7},{7,8},{8,9},{9,10},{10,1... | collective-permute-start | bytes 786440 | tf_op jit(solution)/shard_map/while/body/eval_jaxpr/ppermute | solution.py:17
  120.3 15.7 %collective-permute-start = (f32[1,256,256]{2,1,0:T(8,128)S(1)}, f32[1,256,256]{2,1,0:T(8,128)}, u32[]{:S(2)}, u32[]{:S(2)}) collective-permute-start(f32[1,256,256]{2,1,0:T(8,128)S(1)} %broadcast_select_fusion.2), channel_id=1, source_target_pairs={{1,0},{2,1},{3,2},{4,3},{5,4},{6,5},{7,6},{8,7},{9,8},{10,9},{11,1... | collective-permute-start | bytes 786440 | tf_op jit(solution)/shard_map/while/body/eval_jaxpr/ppermute | solution.py:18
  130.2 5.9 %collective-permute-start.1 = (f32[1,256,256]{2,1,0:T(8,128)S(1)}, f32[1,256,256]{2,1,0:T(8,128)}, u32[]{:S(2)}, u32[]{:S(2)}) collective-permute-start(f32[1,256,256]{2,1,0:T(8,128)S(1)} %broadcast_select_fusion.2), channel_id=1, source_target_pairs={{0,1},{1,2},{2,3},{3,4},{4,5},{5,6},{6,7},{7,8},{8,9},{9,10},{10,1... | collective-permute-start | bytes 786440 | tf_op jit(solution)/shard_map/while/body/eval_jaxpr/ppermute | solution.py:17
  137.7 11.3 %collective-permute-start.2 = (f32[1,256,256]{2,1,0:T(8,128)S(1)}, f32[1,256,256]{2,1,0:T(8,128)S(1)}, u32[]{:S(2)}, u32[]{:S(2)}) collective-permute-start(f32[1,256,256]{2,1,0:T(8,128)S(1)} %fusion.50), channel_id=1, source_target_pairs={{1,0},{2,1},{3,2},{4,3},{5,4},{6,5},{7,6},{8,7},{9,8},{10,9},{11,1... | collective-permute-start | bytes 786440 | tf_op jit(solution)/shard_map/while/body/eval_jaxpr/ppermute | solution.py:18
  146.9 5.2 %collective-permute-start.3 = (f32[1,256,256]{2,1,0:T(8,128)S(1)}, f32[1,256,256]{2,1,0:T(8,128)S(1)}, u32[]{:S(2)}, u32[]{:S(2)}) collective-permute-start(f32[1,256,256]{2,1,0:T(8,128)S(1)} %fusion.50), channel_id=1, source_target_pairs={{0,1},{1,2},{2,3},{3,4},{4,5},{5,6},{6,7},{7,8},{8,9},{9,10},{10,1... | collective-permute-start | bytes 786440 | tf_op jit(solution)/shard_map/while/body/eval_jaxpr/ppermute | solution.py:17
  152.5 15.7 %collective-permute-start = (f32[1,256,256]{2,1,0:T(8,128)S(1)}, f32[1,256,256]{2,1,0:T(8,128)}, u32[]{:S(2)}, u32[]{:S(2)}) collective-permute-start(f32[1,256,256]{2,1,0:T(8,128)S(1)} %broadcast_select_fusion.2), channel_id=1, source_target_pairs={{1,0},{2,1},{3,2},{4,3},{5,4},{6,5},{7,6},{8,7},{9,8},{10,9},{11,1... | collective-permute-start | bytes 786440 | tf_op jit(solution)/shard_map/while/body/eval_jaxpr/ppermute | solution.py:18
  162.4 5.9 %collective-permute-start.1 = (f32[1,256,256]{2,1,0:T(8,128)S(1)}, f32[1,256,256]{2,1,0:T(8,128)}, u32[]{:S(2)}, u32[]{:S(2)}) collective-permute-start(f32[1,256,256]{2,1,0:T(8,128)S(1)} %broadcast_select_fusion.2), channel_id=1, source_target_pairs={{0,1},{1,2},{2,3},{3,4},{4,5},{5,6},{6,7},{7,8},{8,9},{9,10},{10,1... | collective-permute-start | bytes 786440 | tf_op jit(solution)/shard_map/while/body/eval_jaxpr/ppermute | solution.py:17
  169.9 11.3 %collective-permute-start.2 = (f32[1,256,256]{2,1,0:T(8,128)S(1)}, f32[1,256,256]{2,1,0:T(8,128)S(1)}, u32[]{:S(2)}, u32[]{:S(2)}) collective-permute-start(f32[1,256,256]{2,1,0:T(8,128)S(1)} %fusion.50), channel_id=1, source_target_pairs={{1,0},{2,1},{3,2},{4,3},{5,4},{6,5},{7,6},{8,7},{9,8},{10,9},{11,1... | collective-permute-start | bytes 786440 | tf_op jit(solution)/shard_map/while/body/eval_jaxpr/ppermute | solution.py:18
  179.1 5.2 %collective-permute-start.3 = (f32[1,256,256]{2,1,0:T(8,128)S(1)}, f32[1,256,256]{2,1,0:T(8,128)S(1)}, u32[]{:S(2)}, u32[]{:S(2)}) collective-permute-start(f32[1,256,256]{2,1,0:T(8,128)S(1)} %fusion.50), channel_id=1, source_target_pairs={{0,1},{1,2},{2,3},{3,4},{4,5},{5,6},{6,7},{7,8},{8,9},{9,10},{10,1... | collective-permute-start | bytes 786440 | tf_op jit(solution)/shard_map/while/body/eval_jaxpr/ppermute | solution.py:17
  184.7 15.7 %collective-permute-start = (f32[1,256,256]{2,1,0:T(8,128)S(1)}, f32[1,256,256]{2,1,0:T(8,128)}, u32[]{:S(2)}, u32[]{:S(2)}) collective-permute-start(f32[1,256,256]{2,1,0:T(8,128)S(1)} %broadcast_select_fusion.2), channel_id=1, source_target_pairs={{1,0},{2,1},{3,2},{4,3},{5,4},{6,5},{7,6},{8,7},{9,8},{10,9},{11,1... | collective-permute-start | bytes 786440 | tf_op jit(solution)/shard_map/while/body/eval_jaxpr/ppermute | solution.py:18
  194.6 5.9 %collective-permute-start.1 = (f32[1,256,256]{2,1,0:T(8,128)S(1)}, f32[1,256,256]{2,1,0:T(8,128)}, u32[]{:S(2)}, u32[]{:S(2)}) collective-permute-start(f32[1,256,256]{2,1,0:T(8,128)S(1)} %broadcast_select_fusion.2), channel_id=1, source_target_pairs={{0,1},{1,2},{2,3},{3,4},{4,5},{5,6},{6,7},{7,8},{8,9},{9,10},{10,1... | collective-permute-start | bytes 786440 | tf_op jit(solution)/shard_map/while/body/eval_jaxpr/ppermute | solution.py:17
  202.1 11.3 %collective-permute-start.2 = (f32[1,256,256]{2,1,0:T(8,128)S(1)}, f32[1,256,256]{2,1,0:T(8,128)S(1)}, u32[]{:S(2)}, u32[]{:S(2)}) collective-permute-start(f32[1,256,256]{2,1,0:T(8,128)S(1)} %fusion.50), channel_id=1, source_target_pairs={{1,0},{2,1},{3,2},{4,3},{5,4},{6,5},{7,6},{8,7},{9,8},{10,9},{11,1... | collective-permute-start | bytes 786440 | tf_op jit(solution)/shard_map/while/body/eval_jaxpr/ppermute | solution.py:18
  211.3 5.2 %collective-permute-start.3 = (f32[1,256,256]{2,1,0:T(8,128)S(1)}, f32[1,256,256]{2,1,0:T(8,128)S(1)}, u32[]{:S(2)}, u32[]{:S(2)}) collective-permute-start(f32[1,256,256]{2,1,0:T(8,128)S(1)} %fusion.50), channel_id=1, source_target_pairs={{0,1},{1,2},{2,3},{3,4},{4,5},{5,6},{6,7},{7,8},{8,9},{9,10},{10,1... | collective-permute-start | bytes 786440 | tf_op jit(solution)/shard_map/while/body/eval_jaxpr/ppermute | solution.py:17
  216.9 15.7 %collective-permute-start = (f32[1,256,256]{2,1,0:T(8,128)S(1)}, f32[1,256,256]{2,1,0:T(8,128)}, u32[]{:S(2)}, u32[]{:S(2)}) collective-permute-start(f32[1,256,256]{2,1,0:T(8,128)S(1)} %broadcast_select_fusion.2), channel_id=1, source_target_pairs={{1,0},{2,1},{3,2},{4,3},{5,4},{6,5},{7,6},{8,7},{9,8},{10,9},{11,1... | collective-permute-start | bytes 786440 | tf_op jit(solution)/shard_map/while/body/eval_jaxpr/ppermute | solution.py:18
  226.8 5.9 %collective-permute-start.1 = (f32[1,256,256]{2,1,0:T(8,128)S(1)}, f32[1,256,256]{2,1,0:T(8,128)}, u32[]{:S(2)}, u32[]{:S(2)}) collective-permute-start(f32[1,256,256]{2,1,0:T(8,128)S(1)} %broadcast_select_fusion.2), channel_id=1, source_target_pairs={{0,1},{1,2},{2,3},{3,4},{4,5},{5,6},{6,7},{7,8},{8,9},{9,10},{10,1... | collective-permute-start | bytes 786440 | tf_op jit(solution)/shard_map/while/body/eval_jaxpr/ppermute | solution.py:17
  234.3 11.3 %collective-permute-start.2 = (f32[1,256,256]{2,1,0:T(8,128)S(1)}, f32[1,256,256]{2,1,0:T(8,128)S(1)}, u32[]{:S(2)}, u32[]{:S(2)}) collective-permute-start(f32[1,256,256]{2,1,0:T(8,128)S(1)} %fusion.50), channel_id=1, source_target_pairs={{1,0},{2,1},{3,2},{4,3},{5,4},{6,5},{7,6},{8,7},{9,8},{10,9},{11,1... | collective-permute-start | bytes 786440 | tf_op jit(solution)/shard_map/while/body/eval_jaxpr/ppermute | solution.py:18
  249.1 15.7 %collective-permute-start = (f32[1,256,256]{2,1,0:T(8,128)S(1)}, f32[1,256,256]{2,1,0:T(8,128)}, u32[]{:S(2)}, u32[]{:S(2)}) collective-permute-start(f32[1,256,256]{2,1,0:T(8,128)S(1)} %broadcast_select_fusion.2), channel_id=1, source_target_pairs={{1,0},{2,1},{3,2},{4,3},{5,4},{6,5},{7,6},{8,7},{9,8},{10,9},{11,1... | collective-permute-start | bytes 786440 | tf_op jit(solution)/shard_map/while/body/eval_jaxpr/ppermute | solution.py:18
  259.0 5.9 %collective-permute-start.1 = (f32[1,256,256]{2,1,0:T(8,128)S(1)}, f32[1,256,256]{2,1,0:T(8,128)}, u32[]{:S(2)}, u32[]{:S(2)}) collective-permute-start(f32[1,256,256]{2,1,0:T(8,128)S(1)} %broadcast_select_fusion.2), channel_id=1, source_target_pairs={{0,1},{1,2},{2,3},{3,4},{4,5},{5,6},{6,7},{7,8},{8,9},{9,10},{10,1... | collective-permute-start | bytes 786440 | tf_op jit(solution)/shard_map/while/body/eval_jaxpr/ppermute | solution.py:17
  266.5 11.3 %collective-permute-start.2 = (f32[1,256,256]{2,1,0:T(8,128)S(1)}, f32[1,256,256]{2,1,0:T(8,128)S(1)}, u32[]{:S(2)}, u32[]{:S(2)}) collective-permute-start(f32[1,256,256]{2,1,0:T(8,128)S(1)} %fusion.50), channel_id=1, source_target_pairs={{1,0},{2,1},{3,2},{4,3},{5,4},{6,5},{7,6},{8,7},{9,8},{10,9},{11,1... | collective-permute-start | bytes 786440 | tf_op jit(solution)/shard_map/while/body/eval_jaxpr/ppermute | solution.py:18
  281.3 15.7 %collective-permute-start = (f32[1,256,256]{2,1,0:T(8,128)S(1)}, f32[1,256,256]{2,1,0:T(8,128)}, u32[]{:S(2)}, u32[]{:S(2)}) collective-permute-start(f32[1,256,256]{2,1,0:T(8,128)S(1)} %broadcast_select_fusion.2), channel_id=1, source_target_pairs={{1,0},{2,1},{3,2},{4,3},{5,4},{6,5},{7,6},{8,7},{9,8},{10,9},{11,1... | collective-permute-start | bytes 786440 | tf_op jit(solution)/shard_map/while/body/eval_jaxpr/ppermute | solution.py:18
  291.2 5.9 %collective-permute-start.1 = (f32[1,256,256]{2,1,0:T(8,128)S(1)}, f32[1,256,256]{2,1,0:T(8,128)}, u32[]{:S(2)}, u32[]{:S(2)}) collective-permute-start(f32[1,256,256]{2,1,0:T(8,128)S(1)} %broadcast_select_fusion.2), channel_id=1, source_target_pairs={{0,1},{1,2},{2,3},{3,4},{4,5},{5,6},{6,7},{7,8},{8,9},{9,10},{10,1... | collective-permute-start | bytes 786440 | tf_op jit(solution)/shard_map/while/body/eval_jaxpr/ppermute | solution.py:17
  298.7 11.3 %collective-permute-start.2 = (f32[1,256,256]{2,1,0:T(8,128)S(1)}, f32[1,256,256]{2,1,0:T(8,128)S(1)}, u32[]{:S(2)}, u32[]{:S(2)}) collective-permute-start(f32[1,256,256]{2,1,0:T(8,128)S(1)} %fusion.50), channel_id=1, source_target_pairs={{1,0},{2,1},{3,2},{4,3},{5,4},{6,5},{7,6},{8,7},{9,8},{10,9},{11,1... | collective-permute-start | bytes 786440 | tf_op jit(solution)/shard_map/while/body/eval_jaxpr/ppermute | solution.py:18
  313.5 15.7 %collective-permute-start = (f32[1,256,256]{2,1,0:T(8,128)S(1)}, f32[1,256,256]{2,1,0:T(8,128)}, u32[]{:S(2)}, u32[]{:S(2)}) collective-permute-start(f32[1,256,256]{2,1,0:T(8,128)S(1)} %broadcast_select_fusion.2), channel_id=1, source_target_pairs={{1,0},{2,1},{3,2},{4,3},{5,4},{6,5},{7,6},{8,7},{9,8},{10,9},{11,1... | collective-permute-start | bytes 786440 | tf_op jit(solution)/shard_map/while/body/eval_jaxpr/ppermute | solution.py:18
  323.4 5.9 %collective-permute-start.1 = (f32[1,256,256]{2,1,0:T(8,128)S(1)}, f32[1,256,256]{2,1,0:T(8,128)}, u32[]{:S(2)}, u32[]{:S(2)}) collective-permute-start(f32[1,256,256]{2,1,0:T(8,128)S(1)} %broadcast_select_fusion.2), channel_id=1, source_target_pairs={{0,1},{1,2},{2,3},{3,4},{4,5},{5,6},{6,7},{7,8},{8,9},{9,10},{10,1... | collective-permute-start | bytes 786440 | tf_op jit(solution)/shard_map/while/body/eval_jaxpr/ppermute | solution.py:17
  330.9 11.3 %collective-permute-start.2 = (f32[1,256,256]{2,1,0:T(8,128)S(1)}, f32[1,256,256]{2,1,0:T(8,128)S(1)}, u32[]{:S(2)}, u32[]{:S(2)}) collective-permute-start(f32[1,256,256]{2,1,0:T(8,128)S(1)} %fusion.50), channel_id=1, source_target_pairs={{1,0},{2,1},{3,2},{4,3},{5,4},{6,5},{7,6},{8,7},{9,8},{10,9},{11,1... | collective-permute-start | bytes 786440 | tf_op jit(solution)/shard_map/while/body/eval_jaxpr/ppermute | solution.py:18
  345.7 12.4 %collective-permute-start.7 = (f32[1,256,256]{2,1,0:T(8,128)S(1)}, f32[1,256,256]{2,1,0:T(8,128)S(1)}, u32[]{:S(2)}, u32[]{:S(2)}) collective-permute-start(f32[1,256,256]{2,1,0:T(8,128)S(1)} %get-tuple-element.76), channel_id=1, source_target_pairs={{1,0},{2,1},{3,2},{4,3},{5,4},{6,5},{7,6},{8,7},{9,8},{10,9},{11,1... | collective-permute-start | bytes 786440 | tf_op jit(solution)/shard_map/ppermute | solution.py:32
  (18 other events, 238.7 us)
where the time goes:
time: 385 us; the launch traced here: 379 us
  starting transfers between devices  212 us (55%)
  local copies, waits for them, and re-layouts  83 us (22%)
  waiting for transfers between devices  48.3 us (13%)
  other arithmetic  34.3 us (9%)
    ppermute x17, starting transfers between devices, padded_2(): lax.ppermute(initial, axis, [(b, a) for a, b in up])  163 us
    ppermute x17, starting transfers between devices, padded_2(): lax.ppermute(last, axis, up)  33.9 us
    ppermute x17, waiting for transfers between devices, padded_2(): lax.ppermute(last, axis, up)  26.2 us
    slice x2, local copies, waits for them, and re-layouts, restrict_axis(): even_part = lax.slice_in_dim(values, 0, None, 2, direction)  16.7 us
    slice x3, local copies, waits for them, and re-layouts, restrict_axis(): odd_part = lax.slice_in_dim(values, 1, None, 2, direction)  15.5 us
    select_n x16, other arithmetic, one_sweep(): values = jnp.where(update, (forcing + neighbours) / 6.0, values)  15.5 us
    ppermute x2, starting transfers between devices, from_behind(): lax.ppermute(value, axis, [(source, source + steps) for source in range(i...  14.4 us
    ppermute x2, waiting for transfers between devices, from_behind(): lax.ppermute(value, axis, [(source, source + steps) for source in range(i...  11.7 us
  transfers between devices with their start and end apart: 36, of which 11 were waited for; matrix products, arithmetic and copies ran while one was open for 9% of the time, Pallas kernels for 0%

commit v1 on v0

v1 whole, which is shorter than its diff:
```python
import functools

import jax
import jax.numpy as jnp
from jax import lax
from jax.experimental import pallas as pl
from jax.experimental.pallas import tpu as pltpu
from jax.sharding import PartitionSpec as P

F32 = jnp.float32
BF16 = jnp.bfloat16
MESH = pl.DeviceIdType.MESH

NF = 512
NC = 256
MEM = 8
ROWS = NC // MEM
HALO = 8
SLOTS = MEM + 2 * HALO
FROWS = ROWS + 2 * HALO
VROWS = FROWS + 16
CHUNKS = 4
CROWS = NC // CHUNKS
FINE = 2 * CROWS


def iota(shape, dim):
    return lax.broadcasted_iota(jnp.int32, shape, dim)


def split3(x):
    high = x.astype(BF16)
    rest = x - high.astype(F32)
    middle = rest.astype(BF16)
    low = (rest - middle.astype(F32)).astype(BF16)
    return high, middle, low


def dot_exact(x, weights):
    rows = x.shape[0]
    parts = jnp.concatenate(split3(x), axis=0)
    out = jnp.dot(parts, weights, preferred_element_type=F32)
    return out[:rows] + (out[rows : 2 * rows] + out[2 * rows :])


def coarse_column(shape, dim):
    n = iota(shape, dim)
    return jnp.where(n < NC // 2, 2 * n, 2 * n - (NC - 1))


def restrict_kernel(p_hbm, s_hbm, side, end_hbm, out, pb, sb, eb, w_rc, w_lr, w_perm, sems, end_sem):
    groups = lax.axis_size("grp")
    device = lax.axis_index("grp") * MEM + lax.axis_index("mem")
    is_first = device == 0
    is_last = device == groups * MEM - 1

    copies = []
    for c in range(CHUNKS):
        row = []
        for t in range(4):
            for a, (src, dst) in enumerate(((p_hbm, pb), (s_hbm, sb))):
                row.append(
                    pltpu.make_async_copy(
                        src.at[:, pl.ds(FINE * c, FINE), pl.ds(128 * t, 128)],
                        dst.at[:, t, pl.ds(8 + FINE * c, FINE), :],
                        sems.at[c, t, a],
                    )
                )
        copies.append(row)
    for row in copies:
        for copy in row:
            copy.start()
    end_copy = pltpu.make_async_copy(
        end_hbm.at[jnp.where(is_last, 1, 0)], eb, end_sem
    )
    at_end = jnp.logical_or(is_first, is_last)

    @pl.when(at_end)
    def _():
        end_copy.start()

    zeros = jnp.zeros((2, 4, 8, 128), F32)
    pb[:, :, 0:8, :] = zeros
    pb[:, :, 8 + NF : 16 + NF, :] = zeros
    sb[:, :, 0:8, :] = zeros

    column = coarse_column((NF, NC), 1)
    step = jnp.abs(iota((NF, NC), 0) - 2 * column)
    w_rc[...] = jnp.where(step == 0, 0.5, jnp.where(step == 1, 0.25, 0.0)).astype(BF16)
    near = jnp.where(step == 0, jnp.where(column == 0, 0.25, 0.5), 0.5)
    w_lr[...] = jnp.where(step <= 1, near, jnp.where(step == 2, 0.25, 0.0)).astype(BF16)
    square = coarse_column((NC, NC), 1)
    w_perm[...] = jnp.where(iota((NC, NC), 0) == square, 1.0, 0.0).astype(BF16)

    front = dot_exact(jnp.broadcast_to(side[0, 0:1, :], (8, NC)), w_perm[...])[0:1]
    back = dot_exact(jnp.broadcast_to(side[0, 1:2, :], (8, NC)), w_perm[...])[0:1]
    own_weight = jnp.where(is_first, 0.25, 0.5)

    def store(field, c, value):
        row = CROWS * c + iota((CROWS, 128), 0)
        even = lax.rem(row + device + (field > 0), 2) == 0
        left, right = value[:, :128], value[:, 128:]
        red = jnp.where(even, left, right)
        black = jnp.where(even, right, left)
        for b in range(CROWS // ROWS):
            q = c * (CROWS // ROWS) + b
            out[field, q, 0] = red[ROWS * b : ROWS * (b + 1)]
            out[field, q, 1] = black[ROWS * b : ROWS * (b + 1)]

    for copy in copies[0]:
        copy.wait()
    for c in range(CHUNKS):
        if c + 1 < CHUNKS:
            for copy in copies[c + 1]:
                copy.wait()
        fields = [[], [], [], [], []]
        for t in range(4):

            def load(ref, plane, shift):
                return ref[plane, t, pl.ds(8 + FINE * c + shift, CROWS, stride=2), :]

            a, b = [], []
            for plane in (0, 1):
                p_before, p_here, p_after = (load(pb, plane, k) for k in (-1, 0, 1))
                outer = load(pb, plane, -2) + load(pb, plane, 2)
                odd = p_before + p_after
                s_part = 0.5 * load(sb, plane, 0) + 0.25 * (load(sb, plane, -1) + load(sb, plane, 1))
                value = s_part + (outer - 4.0 * odd - 10.0 * p_here)
                if c == 0:
                    value = value - jnp.where(iota(value.shape, 0) == 0, p_here, 0.0)
                a.append(value)
                b.append(2.0 * p_here + odd)
            up = 0.25 * a[1] + 0.5 * b[1]
            fields[0].append(0.5 * a[0] + up + own_weight * b[0])
            fields[1].append(up + 0.25 * b[0])
            fields[2].append(0.25 * b[0])
            fields[3].append(0.5 * b[0] + 0.25 * b[1])
            fields[4].append(0.25 * b[1])
        wide = [jnp.concatenate(f, axis=1) for f in fields]
        plain = dot_exact(jnp.concatenate(wide[:3], axis=0), w_rc[...])
        cross = dot_exact(jnp.concatenate(wide[3:], axis=0), w_lr[...])
        local = plain[:CROWS] + cross[:CROWS]
        above = plain[CROWS : 2 * CROWS] + cross[CROWS:]
        below = plain[2 * CROWS :]
        row = iota((CROWS, NC), 0)
        lane = iota((CROWS, NC), 1)
        diagonal = lane == row + CROWS * c
        left = jnp.sum(jnp.where(diagonal, side[0, 2:3, :], 0.0), axis=1, keepdims=True)
        right = jnp.sum(jnp.where(diagonal, side[0, 3:4, :], 0.0), axis=1, keepdims=True)
        local = local + jnp.where(lane == 0, left, jnp.where(lane == NC - 1, right, 0.0))
        if c == 0:
            local = local + jnp.where(row == 0, front, 0.0)
        if c == CHUNKS - 1:
            local = local + jnp.where(row == CROWS - 1, back, 0.0)
        store(0, c, local)
        store(1, c, above)
        store(2, c, below)

    @pl.when(at_end)
    def _():
        end_copy.wait()
        for c in range(CHUNKS):
            rows = pl.ds(CROWS * c, CROWS)
            face = dot_exact(eb[rows, :], w_perm[...])
            row = CROWS * c + iota((CROWS, 128), 0)
            even = lax.rem(row + device, 2) == 0
            red = jnp.where(even, face[:, :128], face[:, 128:])
            black = jnp.where(even, face[:, 128:], face[:, :128])
            for b in range(CROWS // ROWS):
                q = c * (CROWS // ROWS) + b
                out[0, q, 0] = out[0, q, 0] + red[ROWS * b : ROWS * (b + 1)]
                out[0, q, 1] = out[0, q, 1] + black[ROWS * b : ROWS * (b + 1)]


def restrict(potential, source, side_faces, end_faces):
    anyspace = pl.BlockSpec(memory_space=pl.ANY)
    return pl.pallas_call(
        restrict_kernel,
        out_shape=jax.ShapeDtypeStruct((3, MEM, 2, ROWS, 128), F32),
        in_specs=[anyspace, anyspace, pl.BlockSpec(memory_space=pltpu.VMEM), anyspace],
        out_specs=pl.BlockSpec(memory_space=pltpu.VMEM),
        scratch_shapes=[
            pltpu.VMEM((2, 4, NF + 16, 128), F32),
            pltpu.VMEM((2, 4, NF + 16, 128), F32),
            pltpu.VMEM((NC, NC), F32),
            pltpu.VMEM((NF, NC), BF16),
            pltpu.VMEM((NF, NC), BF16),
            pltpu.VMEM((NC, NC), BF16),
            pltpu.SemaphoreType.DMA((CHUNKS, 4, 2)),
            pltpu.SemaphoreType.DMA,
        ],
        name="restrict",
    )(potential, source, side_faces, end_faces)


DIRECTIONS = tuple((dg, dm) for dg in (-1, 0, 1) for dm in (-1, 0, 1) if (dg, dm) != (0, 0))


def smooth_kernel(
    fields, e_out, partner, summed, fb, xb, vr, vk, vk2,
    partner_sems, f_send, f_recv, x_send, x_recv, h_send, h_recv, b_send, b_recv, e_send, e_recv, e_local,
):
    groups = lax.axis_size("grp")
    g = lax.axis_index("grp")
    m = lax.axis_index("mem")

    def remote(src, dst, send, recv, tg, tm):
        return pltpu.make_async_remote_copy(
            src_ref=src, dst_ref=dst, send_sem=send, recv_sem=recv,
            device_id={"grp": tg, "mem": tm}, device_id_type=MESH,
        )

    vr[...] = jnp.zeros_like(vr)
    vk[...] = jnp.zeros_like(vk)
    vk2[...] = jnp.zeros_like(vk2)
    fb[...] = jnp.zeros_like(fb)
    xb[...] = jnp.zeros_like(xb)

    barrier = pltpu.get_barrier_semaphore()
    for dg in (-1, 0, 1):
        exists = jnp.logical_and(g + dg >= 0, g + dg < groups)

        @pl.when(exists)
        def _():
            for i in range(1 if dg == 0 else 0, MEM):
                pl.semaphore_signal(
                    barrier, inc=1,
                    device_id={"grp": g + dg, "mem": lax.rem(m + i, MEM)}, device_id_type=MESH,
                )
    count = (MEM - 1) + jnp.where(g > 0, MEM, 0) + jnp.where(g < groups - 1, MEM, 0)
    pl.semaphore_wait(barrier, count)

    odd = lax.rem(m, 2)
    to_partner = remote(
        fields.at[1 + odd], partner, partner_sems.at[0], partner_sems.at[1], g, m + 1 - 2 * odd
    )
    to_partner.start()

    x_group = g - jnp.where(m == 0, 1, 0) + jnp.where(m == MEM - 1, 1, 0)
    x_plane = lax.rem(m + jnp.where(odd == 1, 1, MEM - 1), MEM)
    x_field = 2 - odd
    x_valid = jnp.logical_and(x_group >= 0, x_group < groups)
    x_home = x_group == g
    x_copies = []
    for i in range(MEM):
        q = lax.rem(m + i, MEM)
        copy = remote(fields.at[x_field, q], xb.at[x_plane], x_send.at[i], x_recv.at[x_plane], x_group, q)
        sends = jnp.logical_and(x_valid, jnp.logical_not(x_home)) if i == 0 else x_valid
        x_copies.append((copy, sends))

        @pl.when(sends)
        def _():
            copy.start()

    @pl.when(x_home)
    def _():
        xb[x_plane] = fields[x_field, m]

    to_partner.wait_recv()
    summed[...] = fields[0] + partner[...]
    own_rows = pl.ds(HALO, ROWS)
    f_copies = []
    for i in range(1, MEM):
        q = lax.rem(m + i, MEM)
        copy = remote(summed.at[q], fb.at[HALO + m, :, own_rows], f_send.at[i], f_recv.at[m], g, q)
        copy.start()
        f_copies.append(copy)
    fb[HALO + m, :, HALO : HALO + ROWS, :] = summed[m]

    for k in range(MEM):
        @pl.when(m != k)
        def _():
            remote(summed.at[0], fb.at[HALO + k, :, own_rows], f_send.at[0], f_recv.at[k], g, k).wait_recv()

        arrives = jnp.logical_not(jnp.logical_and(x_home, x_plane == k))
        if k == 0:
            arrives = jnp.logical_and(arrives, g > 0)
        if k == MEM - 1:
            arrives = jnp.logical_and(arrives, g < groups - 1)

        @pl.when(arrives)
        def _():
            remote(fields.at[0, 0], xb.at[k], x_send.at[0], x_recv.at[k], g, k).wait_recv()

        fb[HALO + k, :, HALO : HALO + ROWS, :] = fb[HALO + k, :, HALO : HALO + ROWS, :] + xb[k]

    def inside(dg, dm):
        ok = None
        for test in (
            (g + dg >= 0) if dg < 0 else (g + dg < groups) if dg > 0 else None,
            (m + dm >= 0) if dm < 0 else (m + dm < MEM) if dm > 0 else None,
        ):
            if test is not None:
                ok = test if ok is None else jnp.logical_and(ok, test)
        return ok

    def exchange(make):
        copies = []
        for o, (dg, dm) in enumerate(DIRECTIONS):
            copy = make(o, dg, dm)
            copies.append(copy)

            @pl.when(inside(dg, dm))
            def _():
                copy.start()
        return copies

    def arrive(copies):
        for o, (dg, dm) in enumerate(DIRECTIONS):
            @pl.when(inside(-dg, -dm))
            def _():
                copies[o].wait_recv()

    def row_parts(dm, base):
        if dm < 0:
            return pl.ds(base, HALO), pl.ds(base + ROWS, HALO)
        if dm > 0:
            return pl.ds(base + ROWS - HALO, HALO), pl.ds(base - HALO, HALO)
        return pl.ds(base, ROWS), pl.ds(base, ROWS)

    def plane_parts(dg, depth):
        if dg < 0:
            return pl.ds(HALO, depth), pl.ds(HALO + MEM, depth)
        if dg > 0:
            return pl.ds(HALO + MEM - depth, depth), pl.ds(HALO - depth, depth)
        return pl.ds(HALO, MEM), pl.ds(HALO, MEM)

    def forcing_copy(o, dg, dm):
        src_rows, dst_rows = row_parts(dm, HALO)
        src_planes, dst_planes = plane_parts(dg, HALO - 1)
        return remote(
            fb.at[src_planes, :, src_rows], fb.at[dst_planes, :, dst_rows],
            h_send.at[o], h_recv.at[o], g + dg, m + dm,
        )

    def black_copy(o, dg, dm):
        src_rows, dst_rows = row_parts(dm, HALO + 8)
        src_planes, dst_planes = plane_parts(dg, HALO)
        return remote(
            vk2.at[src_planes, src_rows], vk2.at[dst_planes, dst_rows],
            b_send.at[o], b_recv.at[o], g + dg, m + dm,
        )

    h_copies = exchange(forcing_copy)
    arrive(h_copies)

    lane = iota((8, 128), 1)
    row_parity = lax.rem(iota((8, 128), 0), 2)
    sixth = jnp.float32(1.0 / 6.0)
    top_scale = jnp.where(m == 0, jnp.float32(0.0), sixth)
    bottom_scale = jnp.where(m == MEM - 1, jnp.float32(0.0), sixth)

    def half_sweep(colour, low, high, target, source, tiles):
        def plane(slot, carry):
            out = jnp.logical_or(
                jnp.logical_and(slot < HALO, g == 0),
                jnp.logical_and(slot >= HALO + MEM, g == groups - 1),
            )
            flip = lax.rem(slot + colour, 2)
            from_left = row_parity == flip
            keep_left = jnp.logical_and(from_left, lane != 0)
            keep_right = jnp.logical_and(jnp.logical_not(from_left), lane != 127)
            for r in tiles:
                at = 8 + 8 * r
                centre = source[slot, at : at + 8, :]
                beside = jnp.where(
                    keep_left, pltpu.roll(centre, 1, 1),
                    jnp.where(keep_right, pltpu.roll(centre, 127, 1), 0.0),
                )
                rows = source[slot, at - 1 : at + 7, :] + source[slot, at + 1 : at + 9, :]
                depth = source[slot - 1, at : at + 8, :] + source[slot + 1, at : at + 8, :]
                scale = top_scale if r == 0 else bottom_scale if r == FROWS // 8 - 1 else sixth
                scale = jnp.where(out, jnp.float32(0.0), scale)
                total = fb[slot, colour, 8 * r : 8 * r + 8, :] + (depth + (rows + (centre + beside)))
                target[slot, at : at + 8, :] = total * scale
            return carry

        lax.fori_loop(low, high, plane, 0)

    all_tiles = tuple(range(FROWS // 8))
    own_tiles = tuple(range(1, 1 + ROWS // 8))

    def pair(black):
        def body(i, carry):
            half_sweep(0, 1 + 2 * i, SLOTS - 1 - 2 * i, vr, black, all_tiles)
            half_sweep(1, 2 + 2 * i, SLOTS - 2 - 2 * i, black, vr, all_tiles)
            return carry
        return body

    lax.fori_loop(0, 3, pair(vk), 0)
    half_sweep(0, 7, SLOTS - 7, vr, vk, all_tiles)
    half_sweep(1, 8, SLOTS - 8, vk2, vr, own_tiles)
    b_copies = exchange(black_copy)
    arrive(b_copies)
    for o, (dg, dm) in enumerate(DIRECTIONS):
        @pl.when(inside(dg, dm))
        def _():
            b_copies[o].wait_send()
    lax.fori_loop(0, 3, pair(vk2), 0)
    half_sweep(0, 7, SLOTS - 7, vr, vk2, all_tiles)

    v_rows = pl.ds(HALO + 8, ROWS)
    e_copies = []

    def send_back(colour, values):
        for i in range(MEM):
            tm = lax.rem(m + i, MEM)
            if i == 0:
                pltpu.make_async_copy(values.at[HALO + m, v_rows], e_out.at[0, m, colour], e_local.at[0, colour]).start()
            else:
                copy = remote(
                    values.at[HALO + tm, v_rows], e_out.at[0, m, colour],
                    e_send.at[0, colour, i], e_recv.at[0, colour, m], g, tm,
                )
                copy.start()
                e_copies.append((copy, None))
            wraps = tm == MEM - 1
            plane = HALO + jnp.where(wraps, 0, tm + 1)
            tg = g - jnp.where(wraps, 1, 0)
            copy = remote(
                values.at[plane, v_rows], e_out.at[1, m, colour],
                e_send.at[1, colour, i], e_recv.at[1, colour, m], tg, tm,
            )
            if i == 0:
                sends = jnp.logical_and(wraps, g > 0)

                @pl.when(jnp.logical_not(wraps))
                def _():
                    pltpu.make_async_copy(values.at[plane, v_rows], e_out.at[1, m, colour], e_local.at[1, colour]).start()
            else:
                sends = jnp.logical_not(jnp.logical_and(wraps, g == 0))
            e_copies.append((copy, sends))

            @pl.when(sends)
            def _():
                copy.start()

    send_back(0, vr)
    half_sweep(1, 8, SLOTS - 8, vk2, vr, own_tiles)
    send_back(1, vk2)

    to_partner.wait_send()
    for copy, sends in x_copies:
        @pl.when(sends)
        def _():
            copy.wait_send()
    for copy in f_copies:
        copy.wait_send()
    for o, (dg, dm) in enumerate(DIRECTIONS):
        @pl.when(inside(dg, dm))
        def _():
            h_copies[o].wait_send()
    for colour, values in ((0, vr), (1, vk2)):
        pltpu.make_async_copy(values.at[HALO, v_rows], e_out.at[0, m, colour], e_local.at[0, colour]).wait()

        @pl.when(m != MEM - 1)
        def _():
            pltpu.make_async_copy(values.at[HALO, v_rows], e_out.at[1, m, colour], e_local.at[1, colour]).wait()

        for q in range(MEM):
            def wait_for(part):
                remote(
                    values.at[HALO, v_rows], e_out.at[part, q, colour],
                    e_send.at[part, colour, 0], e_recv.at[part, colour, q], g, q,
                ).wait_recv()

            @pl.when(m != q)
            def _():
                wait_for(0)

            last = m == MEM - 1
            arrives = jnp.logical_or(
                jnp.logical_and(jnp.logical_not(last), m != q), jnp.logical_and(last, g < groups - 1)
            )

            @pl.when(arrives)
            def _():
                wait_for(1)
    for copy, sends in e_copies:
        if sends is None:
            copy.wait_send()
        else:
            @pl.when(sends)
            def _():
                copy.wait_send()


def smooth(fields):
    dma = pltpu.SemaphoreType.DMA
    return pl.pallas_call(
        smooth_kernel,
        out_shape=jax.ShapeDtypeStruct((2, MEM, 2, ROWS, 128), F32),
        in_specs=[pl.BlockSpec(memory_space=pltpu.VMEM)],
        out_specs=pl.BlockSpec(memory_space=pl.ANY),
        scratch_shapes=[
            pltpu.VMEM((MEM, 2, ROWS, 128), F32),
            pltpu.VMEM((MEM, 2, ROWS, 128), F32),
            pltpu.VMEM((SLOTS, 2, FROWS, 128), F32),
            pltpu.VMEM((MEM, 2, ROWS, 128), F32),
            pltpu.VMEM((SLOTS, VROWS, 128), F32),
            pltpu.VMEM((SLOTS, VROWS, 128), F32),
            pltpu.VMEM((SLOTS, VROWS, 128), F32),
            dma((2,)),
            dma((MEM,)),
            dma((MEM,)),
            dma((MEM,)),
            dma((MEM,)),
            dma((8,)),
            dma((8,)),
            dma((8,)),
            dma((8,)),
            dma((2, 2, MEM)),
            dma((2, 2, MEM)),
            dma((2, 2)),
        ],
        compiler_params=pltpu.CompilerParams(collective_id=0, has_side_effects=True),
        name="smooth",
    )(fields)


def prolong_kernel(e, p, corrected, correction, w_fine, w_plain):
    groups = lax.axis_size("grp")
    device = lax.axis_index("grp") * MEM + lax.axis_index("mem")
    is_last = device == groups * MEM - 1
    c = pl.program_id(0)
    blocks = CROWS // ROWS

    @pl.when(c == 0)
    def _():
        column = coarse_column((NC, NF), 0)
        fine = iota((NC, NF), 1)
        step = fine - 2 * column
        whole = jnp.logical_or(step == 0, jnp.logical_and(step == 1, column == NC - 1))
        half = jnp.logical_or(step == 1, step == -1)
        w_fine[...] = jnp.where(whole, 1.0, jnp.where(half, 0.5, 0.0)).astype(BF16)
        w_plain[...] = jnp.where(
            iota((NC, NC), 1) == coarse_column((NC, NC), 0), 1.0, 0.0
        ).astype(BF16)

    def by_column(part, shift, red, black):
        row = iota(red.shape, 0)
        even = lax.rem(row + shift + device, 2) == 0
        return jnp.concatenate([jnp.where(even, red, black), jnp.where(even, black, red)], axis=1)

    def rows_of(part):
        here = [by_column(part, part, e[part, c * blocks + b, 0], e[part, c * blocks + b, 1]) for b in range(blocks)]
        q = jnp.minimum(c * blocks + blocks, MEM - 1)
        after = by_column(part, part, e[part, q, 0, 0:8, :], e[part, q, 1, 0:8, :])
        return jnp.concatenate(here, axis=0), after

    here, after = rows_of(0)
    here_up, after_up = rows_of(1)
    at_bottom = c == CHUNKS - 1

    r = iota((FINE, CROWS), 0)
    k = iota((FINE, CROWS), 1)
    last_row = jnp.logical_and(jnp.logical_and(r == FINE - 1, k == CROWS - 1), at_bottom)
    take = jnp.where(
        jnp.logical_or(r == 2 * k, last_row), 1.0,
        jnp.where(jnp.logical_or(r == 2 * k + 1, r == 2 * k - 1), 0.5, 0.0),
    ).astype(BF16)

    def down(x, next_rows):
        parts = jnp.concatenate(split3(x), axis=1)
        out = jnp.dot(take, parts, preferred_element_type=F32)
        out = out[:, :NC] + (out[:, NC : 2 * NC] + out[:, 2 * NC :])
        carry = jnp.where(at_bottom, 0.0, 0.5 * next_rows[0:1, :])
        return out + jnp.where(iota((FINE, NC), 0) == FINE - 1, carry, 0.0)

    above = jnp.where(is_last, here, 0.5 * (here + here_up))
    above_after = jnp.where(is_last, after, 0.5 * (after + after_up))
    corrected[0] = p[0] + dot_exact(down(here, after), w_fine[...])
    corrected[1] = p[1] + dot_exact(down(above, above_after), w_fine[...])
    correction[0] = dot_exact(here, w_plain[...])


def prolong(e, potential):
    return pl.pallas_call(
        prolong_kernel,
        grid=(CHUNKS,),
        out_shape=(
            jax.ShapeDtypeStruct((2, NF, NF), F32),
            jax.ShapeDtypeStruct((1, NC, NC), F32),
        ),
        in_specs=[
            pl.BlockSpec((2, MEM, 2, ROWS, 128), lambda c: (0, 0, 0, 0, 0)),
            pl.BlockSpec((2, FINE, NF), lambda c: (0, c, 0)),
        ],
        out_specs=(
            pl.BlockSpec((2, FINE, NF), lambda c: (0, c, 0)),
            pl.BlockSpec((1, CROWS, NC), lambda c: (0, c, 0)),
        ),
        scratch_shapes=[pltpu.VMEM((NC, NF), BF16), pltpu.VMEM((NC, NC), BF16)],
        name="prolong",
    )(e, potential)


def per_device(potential, source, side_faces, end_faces):
    fields = restrict(potential, source, side_faces, end_faces)
    e = smooth(fields)
    return prolong(e, potential)


def solution(mesh):
    placed = P(("grp", "mem"), None, None)
    return jax.shard_map(
        per_device,
        mesh=mesh,
        in_specs=(placed, placed, placed, P()),
        out_specs=(placed, placed),
        check_vma=False,
    )
```

time: 385 us -> 76.1 us (0.20); the launches traced: 379 us -> 75.4 us
  starting transfers between devices: 212 us -> 0 us
  local copies, waits for them, and re-layouts: 83 us -> 0 us
  Pallas kernels: 0 us -> 74.8 us
  waiting for transfers between devices: 48.3 us -> 0 us
  other arithmetic: 34.3 us -> 0 us
    ppermute x36 -> x0, starting transfers between devices: 212 us -> none  [the longest x17 163 us: padded_2(): lax.ppermute(initial, axis, [(b, a) for a, b in up])]
    pallas_call x0 -> x3, Pallas kernels: none -> 74.8 us  [the longest x1 62.9 us: smooth(): pl.pallas_call(smooth_kernel, out_shape=jax.ShapeDtypeStruct((2, MEM, 2,...]
    slice x48 -> x0, local copies, waits for them, and re-layouts: 55.1 us -> none  [the longest x2 16.7 us: restrict_axis(): even_part = lax.slice_in_dim(values, 0, None, 2, direction)]
    ppermute x36 -> x0, waiting for transfers between devices: 48.3 us -> none  [the longest x17 26.2 us: padded_2(): lax.ppermute(last, axis, up)]
    select_n x16 -> x0, other arithmetic: 15.5 us -> none  [one_sweep(): values = jnp.where(update, (forcing + neighbours) / 6.0, values)]
    concatenate x20 -> x0, local copies, waits for them, and re-layouts: 14.2 us -> none  [the longest x8 6.44 us: side_sum(): left_cells = jnp.concatenate([left_face, values[:, :, :-1]], 2)]
    add x5 -> x0, other arithmetic: 10.3 us -> none  [the longest x3 6.34 us: restrict_axis(): return 0.5 * even_part + 0.25 * (odd_part + earlier)]
    another operation x2 -> x0, local copies, waits for them, and re-layouts: 7.09 us -> none  [prolong_axis(): paired = jnp.stack([values, middle], direction + 1)]
  transfers between devices with their start and end apart: 36 -> 0, of which waited for: 11 -> 0; matrix products, arithmetic and copies ran while one was open for 9% -> 0% of each run, Pallas kernels for 0% -> 0%
where the time goes in v1:
time: 76.1 us; the launch traced here: 75.4 us
  Pallas kernels  74.8 us (98%)
    pallas_call x1, Pallas kernels, smooth(): pl.pallas_call(smooth_kernel, out_shape=jax.ShapeDtypeStruct((2, MEM, 2,...  62.9 us
    pallas_call x1, Pallas kernels, prolong(): pl.pallas_call(prolong_kernel, grid=(CHUNKS,), out_shape=(jax.ShapeDtypeS...  5.98 us
    pallas_call x1, Pallas kernels, restrict(): pl.pallas_call(restrict_kernel, out_shape=jax.ShapeDtypeStruct((3, MEM, 2...  5.86 us

profile of v1, /device:TPU:129, one launch (start us, length us, event | category | flops | bytes accessed | tf_op | source)
XLA Modules:
  0.0 75.4 jit_solution(10597134398394392996)
XLA Ops:
  0.6 5.9 %restrict.1.fields = f32[3,8,2,32,128]{4,3,2,1,0:T(8,128)} custom-call(f32[2,512,512]{2,1,0:T(8,128)} %p.1, f32[2,512,512]{2,1,0:T(8,128)} %s_hbm.1, f32[1,4,256]{2,1,0:T(4,128)} %side.1, f32[2,256,256]{2,1,0:T(8,128)} %end_hbm.1), custom_call_target="tpu_custom_call" | custom-call | tf_op jit(solution)/shard_map/restrict/pallas_call | solution.py:177
  6.5 62.9 %smooth.1.e = f32[2,8,2,32,128]{4,3,2,1,0:T(8,128)} custom-call(f32[3,8,2,32,128]{4,3,2,1,0:T(8,128)} %restrict.1.fields), custom_call_target="tpu_custom_call" | custom-call | tf_op jit(solution)/shard_map/smooth/pallas_call | solution.py:490
  69.4 6.0 %prolong.1 = (f32[2,512,512]{2,1,0:T(8,128)}, f32[1,256,256]{2,1,0:T(8,128)}) custom-call(f32[2,8,2,32,128]{4,3,2,1,0:T(8,128)} %smooth.1.e, f32[2,512,512]{2,1,0:T(8,128)} %p.1), custom_call_target="tpu_custom_call" | custom-call | tf_op jit(solution)/shard_map/prolong/pallas_call | solution.py:578

commit v2 on v1

--- a/solution.py
+++ b/solution.py
@@ -197,7 +197,7 @@
 
 
 def smooth_kernel(
-    fields, e_out, partner, summed, fb, xb, vr, vk, vk2,
+    fields, e_out, partner, summed, fb, xb, vr, vk, vk2, scales,
     partner_sems, f_send, f_recv, x_send, x_recv, h_send, h_recv, b_send, b_recv, e_send, e_recv, e_local,
 ):
     groups = lax.axis_size("grp")
@@ -215,6 +215,12 @@
     vk2[...] = jnp.zeros_like(vk2)
     fb[...] = jnp.zeros_like(fb)
     xb[...] = jnp.zeros_like(xb)
+
+    row = m * ROWS - HALO + iota((FROWS, 128), 0)
+    inner = jnp.where(jnp.logical_and(row >= 0, row < NC), 1.0 / 6.0, 0.0)
+    scales[0] = jnp.where(g > 0, inner, 0.0)
+    scales[1] = inner
+    scales[2] = jnp.where(g < groups - 1, inner, 0.0)
 
     barrier = pltpu.get_barrier_semaphore()
     for dg in (-1, 0, 1):
@@ -346,58 +352,44 @@
 
     lane = iota((8, 128), 1)
     row_parity = lax.rem(iota((8, 128), 0), 2)
-    sixth = jnp.float32(1.0 / 6.0)
-    top_scale = jnp.where(m == 0, jnp.float32(0.0), sixth)
-    bottom_scale = jnp.where(m == MEM - 1, jnp.float32(0.0), sixth)
-
-    def half_sweep(colour, low, high, target, source, tiles):
-        def plane(slot, carry):
-            out = jnp.logical_or(
-                jnp.logical_and(slot < HALO, g == 0),
-                jnp.logical_and(slot >= HALO + MEM, g == groups - 1),
+    from_left = [
+        (jnp.logical_and(row_parity == flip, lane != 0), jnp.logical_and(row_parity != flip, lane != 127))
+        for flip in (0, 1)
+    ]
+
+    def half_sweep(colour, t, target, source, first=0, tiles=FROWS // 8):
+        at, n = 8 + 8 * first, 8 * tiles
+        shape = (tiles, 8, 128)
+        for slot in range(t, SLOTS - t):
+            centre = source[slot, at : at + n, :].reshape(shape)
+            keep_left, keep_right = from_left[(slot + colour) % 2]
+            beside = jnp.where(
+                jnp.broadcast_to(keep_left, shape), pltpu.roll(centre, 1, 2),
+                jnp.where(jnp.broadcast_to(keep_right, shape), pltpu.roll(centre, 127, 2), 0.0),
             )
-            flip = lax.rem(slot + colour, 2)
-            from_left = row_parity == flip
-            keep_left = jnp.logical_and(from_left, lane != 0)
-            keep_right = jnp.logical_and(jnp.logical_not(from_left), lane != 127)
-            for r in tiles:
-                at = 8 + 8 * r
-                centre = source[slot, at : at + 8, :]
-                beside = jnp.where(
-                    keep_left, pltpu.roll(centre, 1, 1),
-                    jnp.where(keep_right, pltpu.roll(centre, 127, 1), 0.0),
-                )
-                rows = source[slot, at - 1 : at + 7, :] + source[slot, at + 1 : at + 9, :]
-                depth = source[slot - 1, at : at + 8, :] + source[slot + 1, at : at + 8, :]
-                scale = top_scale if r == 0 else bottom_scale if r == FROWS // 8 - 1 else sixth
-                scale = jnp.where(out, jnp.float32(0.0), scale)
-                total = fb[slot, colour, 8 * r : 8 * r + 8, :] + (depth + (rows + (centre + beside)))
-                target[slot, at : at + 8, :] = total * scale
-            return carry
-
-        lax.fori_loop(low, high, plane, 0)
-
-    all_tiles = tuple(range(FROWS // 8))
-    own_tiles = tuple(range(1, 1 + ROWS // 8))
-
-    def pair(black):
-        def body(i, carry):
-            half_sweep(0, 1 + 2 * i, SLOTS - 1 - 2 * i, vr, black, all_tiles)
-            half_sweep(1, 2 + 2 * i, SLOTS - 2 - 2 * i, black, vr, all_tiles)
-            return carry
-        return body
-
-    lax.fori_loop(0, 3, pair(vk), 0)
-    half_sweep(0, 7, SLOTS - 7, vr, vk, all_tiles)
-    half_sweep(1, 8, SLOTS - 8, vk2, vr, own_tiles)
+            rows = source[slot, at - 1 : at - 1 + n, :] + source[slot, at + 1 : at + 1 + n, :]
+            depth = source[slot - 1, at : at + n, :] + source[slot + 1, at : at + n, :]
+            side = 0 if slot < HALO else 2 if slot >= HALO + MEM else 1
+            near = (depth + rows).reshape(shape) + (centre + beside)
+            total = fb[slot, colour, 8 * first : 8 * first + n, :].reshape(shape) + near
+            total = total * scales[side, 8 * first : 8 * first + n, :].reshape(shape)
+            target[slot, at : at + n, :] = total.reshape(n, 128)
+
+    def sweeps(black):
+        for t in (1, 3, 5):
+            half_sweep(0, t, vr, black)
+            half_sweep(1, t + 1, black, vr)
+        half_sweep(0, 7, vr, black)
+
+    sweeps(vk)
+    half_sweep(1, 8, vk2, vr, 1, ROWS // 8)
     b_copies = exchange(black_copy)
     arrive(b_copies)
     for o, (dg, dm) in enumerate(DIRECTIONS):
         @pl.when(inside(dg, dm))
         def _():
             b_copies[o].wait_send()
-    lax.fori_loop(0, 3, pair(vk2), 0)
-    half_sweep(0, 7, SLOTS - 7, vr, vk2, all_tiles)
+    sweeps(vk2)
 
     v_rows = pl.ds(HALO + 8, ROWS)
     e_copies = []
@@ -436,7 +428,7 @@
                 copy.start()
 
     send_back(0, vr)
-    half_sweep(1, 8, SLOTS - 8, vk2, vr, own_tiles)
+    half_sweep(1, 8, vk2, vr, 1, ROWS // 8)
     send_back(1, vk2)
 
     to_partner.wait_send()
@@ -500,6 +492,7 @@
             pltpu.VMEM((SLOTS, VROWS, 128), F32),
             pltpu.VMEM((SLOTS, VROWS, 128), F32),
             pltpu.VMEM((SLOTS, VROWS, 128), F32),
+            pltpu.VMEM((3, FROWS, 128), F32),
             dma((2,)),
             dma((MEM,)),
             dma((MEM,)),

time: 76.1 us -> 59.3 us (0.78)
  Pallas kernels: 74.8 us -> 57.9 us
    pallas_call x1, Pallas kernels: 62.9 us -> 46.1 us  [smooth(): pl.pallas_call(smooth_kernel, out_shape=jax.ShapeDtypeStruct((2, MEM, 2,...]
where the time goes in v2:
time: 59.3 us; the launch traced here: 58.6 us
  Pallas kernels  57.9 us (98%)
  between operations  0.65 us (1%)
    pallas_call x1, Pallas kernels, smooth(): pl.pallas_call(smooth_kernel, out_shape=jax.ShapeDtypeStruct((2, MEM, 2,...  46.1 us
    pallas_call x1, Pallas kernels, prolong(): pl.pallas_call(prolong_kernel, grid=(CHUNKS,), out_shape=(jax.ShapeDtypeS...  5.97 us
    pallas_call x1, Pallas kernels, restrict(): pl.pallas_call(restrict_kernel, out_shape=jax.ShapeDtypeStruct((3, MEM, 2...  5.86 us

profile of v2, /device:TPU:129, one launch (start us, length us, event | category | flops | bytes accessed | tf_op | source)
XLA Modules:
  0.0 58.6 jit_solution(17842633044530072306)
XLA Ops:
  0.6 5.9 %restrict.1.fields = f32[3,8,2,32,128]{4,3,2,1,0:T(8,128)} custom-call(f32[2,512,512]{2,1,0:T(8,128)} %p.1, f32[2,512,512]{2,1,0:T(8,128)} %s_hbm.1, f32[1,4,256]{2,1,0:T(4,128)} %side.1, f32[2,256,256]{2,1,0:T(8,128)} %end_hbm.1), custom_call_target="tpu_custom_call" | custom-call | tf_op jit(solution)/shard_map/restrict/pallas_call | solution.py:177
  6.5 46.1 %smooth.1.e = f32[2,8,2,32,128]{4,3,2,1,0:T(8,128)} custom-call(f32[3,8,2,32,128]{4,3,2,1,0:T(8,128)} %restrict.1.fields), custom_call_target="tpu_custom_call" | custom-call | tf_op jit(solution)/shard_map/smooth/pallas_call | solution.py:482
  52.6 6.0 %prolong.1 = (f32[2,512,512]{2,1,0:T(8,128)}, f32[1,256,256]{2,1,0:T(8,128)}) custom-call(f32[2,8,2,32,128]{4,3,2,1,0:T(8,128)} %smooth.1.e, f32[2,512,512]{2,1,0:T(8,128)} %p.1), custom_call_target="tpu_custom_call" | custom-call | tf_op jit(solution)/shard_map/prolong/pallas_call | solution.py:571

commit v3 on v2

--- a/solution.py
+++ b/solution.py
@@ -1,5 +1,3 @@
-import functools
-
 import jax
 import jax.numpy as jnp
 from jax import lax
@@ -48,36 +46,68 @@
     return jnp.where(n < NC // 2, 2 * n, 2 * n - (NC - 1))
 
 
-def restrict_kernel(p_hbm, s_hbm, side, end_hbm, out, pb, sb, eb, w_rc, w_lr, w_perm, sems, end_sem):
+DIRECTIONS = tuple((dg, dm) for dg in (-1, 0, 1) for dm in (-1, 0, 1) if (dg, dm) != (0, 0))
+
+
+def smooth_kernel(
+    p_hbm, s_hbm, side, end_hbm, e_out,
+    pb, sb, eb, w_rc, w_lr, w_perm, fields, partner, summed, fb, xb, vr, vk, vk2, scales,
+    in_sems, end_sem, p_send, p_recv, f_send, f_recv, x_send, x_recv, h_send, h_recv, b_send, b_recv,
+    e_send, e_recv, e_local,
+):
     groups = lax.axis_size("grp")
-    device = lax.axis_index("grp") * MEM + lax.axis_index("mem")
+    g = lax.axis_index("grp")
+    m = lax.axis_index("mem")
+    device = g * MEM + m
     is_first = device == 0
     is_last = device == groups * MEM - 1
-
-    copies = []
-    for c in range(CHUNKS):
-        row = []
-        for t in range(4):
-            for a, (src, dst) in enumerate(((p_hbm, pb), (s_hbm, sb))):
-                row.append(
-                    pltpu.make_async_copy(
-                        src.at[:, pl.ds(FINE * c, FINE), pl.ds(128 * t, 128)],
-                        dst.at[:, t, pl.ds(8 + FINE * c, FINE), :],
-                        sems.at[c, t, a],
-                    )
+    at_end = jnp.logical_or(is_first, is_last)
+
+    def remote(src, dst, send, recv, tg, tm):
+        return pltpu.make_async_remote_copy(
+            src_ref=src, dst_ref=dst, send_sem=send, recv_sem=recv,
+            device_id={"grp": tg, "mem": tm}, device_id_type=MESH,
+        )
+
+    in_copies = []
+    for t in range(4):
+        for a, (src, dst) in enumerate(((p_hbm, pb), (s_hbm, sb))):
+            in_copies.append(
+                pltpu.make_async_copy(
+                    src.at[:, :, pl.ds(128 * t, 128)], dst.at[:, t, pl.ds(8, NF), :], in_sems.at[t, a]
                 )
-        copies.append(row)
-    for row in copies:
-        for copy in row:
-            copy.start()
-    end_copy = pltpu.make_async_copy(
-        end_hbm.at[jnp.where(is_last, 1, 0)], eb, end_sem
-    )
-    at_end = jnp.logical_or(is_first, is_last)
+            )
+    for copy in in_copies:
+        copy.start()
+    end_copy = pltpu.make_async_copy(end_hbm.at[jnp.where(is_last, 1, 0)], eb, end_sem)
 
     @pl.when(at_end)
     def _():
         end_copy.start()
+
+    vk2[...] = jnp.zeros_like(vk2)
+    fb[...] = jnp.zeros_like(fb)
+    xb[...] = jnp.zeros_like(xb)
+
+    barrier = pltpu.get_barrier_semaphore()
+    for dg in (-1, 0, 1):
+        exists = jnp.logical_and(g + dg >= 0, g + dg < groups)
+
+        @pl.when(exists)
+        def _():
+            for i in range(1 if dg == 0 else 0, MEM):
+                pl.semaphore_signal(
+                    barrier, inc=1,
+                    device_id={"grp": g + dg, "mem": lax.rem(m + i, MEM)}, device_id_type=MESH,
+                )
+
+    vr[...] = jnp.zeros_like(vr)
+    vk[...] = jnp.zeros_like(vk)
+    row = m * ROWS - HALO + iota((FROWS, 128), 0)
+    inner = jnp.where(jnp.logical_and(row >= 0, row < NC), 1.0 / 6.0, 0.0)
+    scales[0] = jnp.where(g > 0, inner, 0.0)
+    scales[1] = inner
+    scales[2] = jnp.where(g < groups - 1, inner, 0.0)
 
     zeros = jnp.zeros((2, 4, 8, 128), F32)
     pb[:, :, 0:8, :] = zeros
@@ -95,25 +125,19 @@
     front = dot_exact(jnp.broadcast_to(side[0, 0:1, :], (8, NC)), w_perm[...])[0:1]
     back = dot_exact(jnp.broadcast_to(side[0, 1:2, :], (8, NC)), w_perm[...])[0:1]
     own_weight = jnp.where(is_first, 0.25, 0.5)
-
-    def store(field, c, value):
+    for copy in in_copies:
+        copy.wait()
+
+    blocks = CROWS // ROWS
+
+    def by_colour(value, shift):
+        even = lax.rem(iota((CROWS, 128), 0) + device + shift, 2) == 0
+        left, right = value[:, :128], value[:, 128:]
+        return jnp.where(even, left, right), jnp.where(even, right, left)
+
+    def restrict(c):
+        lists = [[], [], [], [], []]
         row = CROWS * c + iota((CROWS, 128), 0)
-        even = lax.rem(row + device + (field > 0), 2) == 0
-        left, right = value[:, :128], value[:, 128:]
-        red = jnp.where(even, left, right)
-        black = jnp.where(even, right, left)
-        for b in range(CROWS // ROWS):
-            q = c * (CROWS // ROWS) + b
-            out[field, q, 0] = red[ROWS * b : ROWS * (b + 1)]
-            out[field, q, 1] = black[ROWS * b : ROWS * (b + 1)]
-
-    for copy in copies[0]:
-        copy.wait()
-    for c in range(CHUNKS):
-        if c + 1 < CHUNKS:
-            for copy in copies[c + 1]:
-                copy.wait()
-        fields = [[], [], [], [], []]
         for t in range(4):
 
             def load(ref, plane, shift):
@@ -126,169 +150,109 @@
                 odd = p_before + p_after
                 s_part = 0.5 * load(sb, plane, 0) + 0.25 * (load(sb, plane, -1) + load(sb, plane, 1))
                 value = s_part + (outer - 4.0 * odd - 10.0 * p_here)
-                if c == 0:
-                    value = value - jnp.where(iota(value.shape, 0) == 0, p_here, 0.0)
-                a.append(value)
+                a.append(value - jnp.where(row == 0, p_here, 0.0))
                 b.append(2.0 * p_here + odd)
             up = 0.25 * a[1] + 0.5 * b[1]
-            fields[0].append(0.5 * a[0] + up + own_weight * b[0])
-            fields[1].append(up + 0.25 * b[0])
-            fields[2].append(0.25 * b[0])
-            fields[3].append(0.5 * b[0] + 0.25 * b[1])
-            fields[4].append(0.25 * b[1])
-        wide = [jnp.concatenate(f, axis=1) for f in fields]
+            lists[0].append(0.5 * a[0] + up + own_weight * b[0])
+            lists[1].append(up + 0.25 * b[0])
+            lists[2].append(0.25 * b[0])
+            lists[3].append(0.5 * b[0] + 0.25 * b[1])
+            lists[4].append(0.25 * b[1])
+        wide = [jnp.concatenate(f, axis=1) for f in lists]
         plain = dot_exact(jnp.concatenate(wide[:3], axis=0), w_rc[...])
         cross = dot_exact(jnp.concatenate(wide[3:], axis=0), w_lr[...])
         local = plain[:CROWS] + cross[:CROWS]
         above = plain[CROWS : 2 * CROWS] + cross[CROWS:]
         below = plain[2 * CROWS :]
-        row = iota((CROWS, NC), 0)
+        row = CROWS * c + iota((CROWS, NC), 0)
         lane = iota((CROWS, NC), 1)
-        diagonal = lane == row + CROWS * c
-        left = jnp.sum(jnp.where(diagonal, side[0, 2:3, :], 0.0), axis=1, keepdims=True)
-        right = jnp.sum(jnp.where(diagonal, side[0, 3:4, :], 0.0), axis=1, keepdims=True)
+        left = jnp.sum(jnp.where(lane == row, side[0, 2:3, :], 0.0), axis=1, keepdims=True)
+        right = jnp.sum(jnp.where(lane == row, side[0, 3:4, :], 0.0), axis=1, keepdims=True)
         local = local + jnp.where(lane == 0, left, jnp.where(lane == NC - 1, right, 0.0))
-        if c == 0:
-            local = local + jnp.where(row == 0, front, 0.0)
-        if c == CHUNKS - 1:
-            local = local + jnp.where(row == CROWS - 1, back, 0.0)
-        store(0, c, local)
-        store(1, c, above)
-        store(2, c, below)
-
-    @pl.when(at_end)
-    def _():
-        end_copy.wait()
-        for c in range(CHUNKS):
-            rows = pl.ds(CROWS * c, CROWS)
-            face = dot_exact(eb[rows, :], w_perm[...])
-            row = CROWS * c + iota((CROWS, 128), 0)
-            even = lax.rem(row + device, 2) == 0
-            red = jnp.where(even, face[:, :128], face[:, 128:])
-            black = jnp.where(even, face[:, 128:], face[:, :128])
-            for b in range(CROWS // ROWS):
-                q = c * (CROWS // ROWS) + b
-                out[0, q, 0] = out[0, q, 0] + red[ROWS * b : ROWS * (b + 1)]
-                out[0, q, 1] = out[0, q, 1] + black[ROWS * b : ROWS * (b + 1)]
-
-
-def restrict(potential, source, side_faces, end_faces):
-    anyspace = pl.BlockSpec(memory_space=pl.ANY)
-    return pl.pallas_call(
-        restrict_kernel,
-        out_shape=jax.ShapeDtypeStruct((3, MEM, 2, ROWS, 128), F32),
-        in_specs=[anyspace, anyspace, pl.BlockSpec(memory_space=pltpu.VMEM), anyspace],
-        out_specs=pl.BlockSpec(memory_space=pltpu.VMEM),
-        scratch_shapes=[
-            pltpu.VMEM((2, 4, NF + 16, 128), F32),
-            pltpu.VMEM((2, 4, NF + 16, 128), F32),
-            pltpu.VMEM((NC, NC), F32),
-            pltpu.VMEM((NF, NC), BF16),
-            pltpu.VMEM((NF, NC), BF16),
-            pltpu.VMEM((NC, NC), BF16),
-            pltpu.SemaphoreType.DMA((CHUNKS, 4, 2)),
-            pltpu.SemaphoreType.DMA,
-        ],
-        name="restrict",
-    )(potential, source, side_faces, end_faces)
-
-
-DIRECTIONS = tuple((dg, dm) for dg in (-1, 0, 1) for dm in (-1, 0, 1) if (dg, dm) != (0, 0))
-
-
-def smooth_kernel(
-    fields, e_out, partner, summed, fb, xb, vr, vk, vk2, scales,
-    partner_sems, f_send, f_recv, x_send, x_recv, h_send, h_recv, b_send, b_recv, e_send, e_recv, e_local,
-):
-    groups = lax.axis_size("grp")
-    g = lax.axis_index("grp")
-    m = lax.axis_index("mem")
-
-    def remote(src, dst, send, recv, tg, tm):
-        return pltpu.make_async_remote_copy(
-            src_ref=src, dst_ref=dst, send_sem=send, recv_sem=recv,
-            device_id={"grp": tg, "mem": tm}, device_id_type=MESH,
-        )
-
-    vr[...] = jnp.zeros_like(vr)
-    vk[...] = jnp.zeros_like(vk)
-    vk2[...] = jnp.zeros_like(vk2)
-    fb[...] = jnp.zeros_like(fb)
-    xb[...] = jnp.zeros_like(xb)
-
-    row = m * ROWS - HALO + iota((FROWS, 128), 0)
-    inner = jnp.where(jnp.logical_and(row >= 0, row < NC), 1.0 / 6.0, 0.0)
-    scales[0] = jnp.where(g > 0, inner, 0.0)
-    scales[1] = inner
-    scales[2] = jnp.where(g < groups - 1, inner, 0.0)
-
-    barrier = pltpu.get_barrier_semaphore()
-    for dg in (-1, 0, 1):
-        exists = jnp.logical_and(g + dg >= 0, g + dg < groups)
-
-        @pl.when(exists)
-        def _():
-            for i in range(1 if dg == 0 else 0, MEM):
-                pl.semaphore_signal(
-                    barrier, inc=1,
-                    device_id={"grp": g + dg, "mem": lax.rem(m + i, MEM)}, device_id_type=MESH,
-                )
-    count = (MEM - 1) + jnp.where(g > 0, MEM, 0) + jnp.where(g < groups - 1, MEM, 0)
-    pl.semaphore_wait(barrier, count)
+        local = local + jnp.where(row == 0, front, jnp.where(row == NC - 1, back, 0.0))
+        for field, value in ((0, local), (1, above), (2, below)):
+            for colour, part in enumerate(by_colour(value, int(field > 0))):
+                for b in range(blocks):
+                    fields[field, c * blocks + b, colour] = part[ROWS * b : ROWS * (b + 1)]
+
+    def add_end_face(c):
+        face = dot_exact(eb[pl.ds(pl.multiple_of(CROWS * c, CROWS), CROWS), :], w_perm[...])
+        for colour, part in enumerate(by_colour(face, 0)):
+            for b in range(blocks):
+                q = c * blocks + b
+                fields[0, q, colour] = fields[0, q, colour] + part[ROWS * b : ROWS * (b + 1)]
 
     odd = lax.rem(m, 2)
-    to_partner = remote(
-        fields.at[1 + odd], partner, partner_sems.at[0], partner_sems.at[1], g, m + 1 - 2 * odd
-    )
-    to_partner.start()
-
     x_group = g - jnp.where(m == 0, 1, 0) + jnp.where(m == MEM - 1, 1, 0)
     x_plane = lax.rem(m + jnp.where(odd == 1, 1, MEM - 1), MEM)
     x_field = 2 - odd
     x_valid = jnp.logical_and(x_group >= 0, x_group < groups)
     x_home = x_group == g
-    x_copies = []
-    for i in range(MEM):
-        q = lax.rem(m + i, MEM)
-        copy = remote(fields.at[x_field, q], xb.at[x_plane], x_send.at[i], x_recv.at[x_plane], x_group, q)
-        sends = jnp.logical_and(x_valid, jnp.logical_not(x_home)) if i == 0 else x_valid
-        x_copies.append((copy, sends))
-
-        @pl.when(sends)
+    own_rows = pl.ds(HALO, ROWS)
+    sent = []
+
+    def send_if(condition, copy):
+        sent.append((condition, copy))
+
+        @pl.when(condition)
         def _():
             copy.start()
 
-    @pl.when(x_home)
+    def send_fields(i, c):
+        part = pl.ds(c * blocks, blocks)
+        copy = remote(
+            fields.at[1 + odd, part], partner.at[part], p_send.at[i], p_recv.at[i], g, m + 1 - 2 * odd
+        )
+        copy.start()
+        for b in range(blocks):
+            q = c * blocks + b
+            home = jnp.logical_and(x_home, q == m)
+            send_if(
+                jnp.logical_and(x_valid, jnp.logical_not(home)),
+                remote(
+                    fields.at[x_field, q], xb.at[x_plane], x_send.at[i, b], x_recv.at[x_plane], x_group, q
+                ),
+            )
+
+            @pl.when(home)
+            def _():
+                xb[x_plane] = fields[x_field, q]
+        return copy
+
+    def send_sums(i, c, to_partner):
+        to_partner.wait_recv()
+        for b in range(blocks):
+            q = c * blocks + b
+            summed[q] = fields[0, q] + partner[q]
+            send_if(
+                q != m,
+                remote(summed.at[q], fb.at[HALO + m, :, own_rows], f_send.at[i, b], f_recv.at[m], g, q),
+            )
+
+            @pl.when(q == m)
+            def _():
+                fb[HALO + m, :, HALO : HALO + ROWS, :] = summed[q]
+
+    @pl.when(at_end)
     def _():
-        xb[x_plane] = fields[x_field, m]
-
-    to_partner.wait_recv()
-    summed[...] = fields[0] + partner[...]
-    own_rows = pl.ds(HALO, ROWS)
-    f_copies = []
-    for i in range(1, MEM):
-        q = lax.rem(m + i, MEM)
-        copy = remote(summed.at[q], fb.at[HALO + m, :, own_rows], f_send.at[i], f_recv.at[m], g, q)
-        copy.start()
-        f_copies.append(copy)
-    fb[HALO + m, :, HALO : HALO + ROWS, :] = summed[m]
-
-    for k in range(MEM):
-        @pl.when(m != k)
-        def _():
-            remote(summed.at[0], fb.at[HALO + k, :, own_rows], f_send.at[0], f_recv.at[k], g, k).wait_recv()
-
-        arrives = jnp.logical_not(jnp.logical_and(x_home, x_plane == k))
-        if k == 0:
-            arrives = jnp.logical_and(arrives, g > 0)
-        if k == MEM - 1:
-            arrives = jnp.logical_and(arrives, g < groups - 1)
-
-        @pl.when(arrives)
-        def _():
-            remote(fields.at[0, 0], xb.at[k], x_send.at[0], x_recv.at[k], g, k).wait_recv()
-
-        fb[HALO + k, :, HALO : HALO + ROWS, :] = fb[HALO + k, :, HALO : HALO + ROWS, :] + xb[k]
+        end_copy.wait()
+
+    partners = []
+    for i in range(CHUNKS):
+        c = lax.rem(m // blocks + 1 + i, CHUNKS)
+        restrict(c)
+
+        @pl.when(at_end)
+        def _():
+            add_end_face(c)
+
+        if i == 0:
+            count = (MEM - 1) + jnp.where(g > 0, MEM, 0) + jnp.where(g < groups - 1, MEM, 0)
+            pl.semaphore_wait(barrier, count)
+        partners.append(send_fields(i, c))
+        if i > 0:
+            send_sums(i - 1, lax.rem(m // blocks + i, CHUNKS), partners[i - 1])
+    send_sums(CHUNKS - 1, m // blocks, partners[-1])
 
     def inside(dg, dm):
         ok = None
@@ -331,23 +295,55 @@
             return pl.ds(HALO + MEM - depth, depth), pl.ds(HALO - depth, depth)
         return pl.ds(HALO, MEM), pl.ds(HALO, MEM)
 
-    def forcing_copy(o, dg, dm):
+    def forcing_copy(o, dg, dm, k=None):
         src_rows, dst_rows = row_parts(dm, HALO)
-        src_planes, dst_planes = plane_parts(dg, HALO - 1)
+        if k is None:
+            src, dst = plane_parts(dg, HALO - 1 - abs(dm))
+        else:
+            src, dst = HALO + k, HALO + k - MEM * dg
         return remote(
-            fb.at[src_planes, :, src_rows], fb.at[dst_planes, :, dst_rows],
-            h_send.at[o], h_recv.at[o], g + dg, m + dm,
+            fb.at[src, :, src_rows], fb.at[dst, :, dst_rows], h_send.at[o], h_recv.at[o], g + dg, m + dm
         )
+
+    def receive(n, carry):
+        k = lax.rem(m // blocks * blocks + 2 * MEM - blocks * (1 + n // blocks) + lax.rem(n, blocks), MEM)
+
+        @pl.when(m != k)
+        def _():
+            remote(summed.at[0], fb.at[HALO + k, :, own_rows], f_send.at[0, 0], f_recv.at[k], g, k).wait_recv()
+
+        arrives = jnp.logical_not(jnp.logical_and(x_home, x_plane == k))
+        arrives = jnp.logical_and(arrives, jnp.logical_or(k > 0, g > 0))
+        arrives = jnp.logical_and(arrives, jnp.logical_or(k < MEM - 1, g < groups - 1))
+
+        @pl.when(arrives)
+        def _():
+            remote(fields.at[0, 0], xb.at[k], x_send.at[0, 0], x_recv.at[k], g, k).wait_recv()
+
+        fb[HALO + k, :, HALO : HALO + ROWS, :] = fb[HALO + k, :, HALO : HALO + ROWS, :] + xb[k]
+        for o, (dg, dm) in enumerate(DIRECTIONS):
+            depth = HALO - 1 - abs(dm)
+            needed = inside(dg, dm)
+            if dg < 0:
+                needed = jnp.logical_and(needed, k < depth)
+            if dg > 0:
+                needed = jnp.logical_and(needed, k >= MEM - depth)
+
+            @pl.when(needed)
+            def _():
+                forcing_copy(o, dg, dm, k).start()
+        return carry
 
     def black_copy(o, dg, dm):
         src_rows, dst_rows = row_parts(dm, HALO + 8)
-        src_planes, dst_planes = plane_parts(dg, HALO)
+        src_planes, dst_planes = plane_parts(dg, HALO - abs(dm))
         return remote(
             vk2.at[src_planes, src_rows], vk2.at[dst_planes, dst_rows],
             b_send.at[o], b_recv.at[o], g + dg, m + dm,
         )
 
-    h_copies = exchange(forcing_copy)
+    lax.fori_loop(0, MEM, receive, 0)
+    h_copies = [forcing_copy(o, dg, dm) for o, (dg, dm) in enumerate(DIRECTIONS)]
     arrive(h_copies)
 
     lane = iota((8, 128), 1)
@@ -431,13 +427,12 @@
     half_sweep(1, 8, vk2, vr, 1, ROWS // 8)
     send_back(1, vk2)
 
-    to_partner.wait_send()
-    for copy, sends in x_copies:
-        @pl.when(sends)
+    for copy in partners:
+        copy.wait_send()
+    for condition, copy in sent:
+        @pl.when(condition)
         def _():
             copy.wait_send()
-    for copy in f_copies:
-        copy.wait_send()
     for o, (dg, dm) in enumerate(DIRECTIONS):
         @pl.when(inside(dg, dm))
         def _():
@@ -477,14 +472,22 @@
                 copy.wait_send()
 
 
-def smooth(fields):
+def smooth(potential, source, side_faces, end_faces):
     dma = pltpu.SemaphoreType.DMA
+    anyspace = pl.BlockSpec(memory_space=pl.ANY)
     return pl.pallas_call(
         smooth_kernel,
         out_shape=jax.ShapeDtypeStruct((2, MEM, 2, ROWS, 128), F32),
-        in_specs=[pl.BlockSpec(memory_space=pltpu.VMEM)],
-        out_specs=pl.BlockSpec(memory_space=pl.ANY),
+        in_specs=[anyspace, anyspace, pl.BlockSpec(memory_space=pltpu.VMEM), anyspace],
+        out_specs=anyspace,
         scratch_shapes=[
+            pltpu.VMEM((2, 4, NF + 16, 128), F32),
+            pltpu.VMEM((2, 4, NF + 16, 128), F32),
+            pltpu.VMEM((NC, NC), F32),
+            pltpu.VMEM((NF, NC), BF16),
+            pltpu.VMEM((NF, NC), BF16),
+            pltpu.VMEM((NC, NC), BF16),
+            pltpu.VMEM((3, MEM, 2, ROWS, 128), F32),
             pltpu.VMEM((MEM, 2, ROWS, 128), F32),
             pltpu.VMEM((MEM, 2, ROWS, 128), F32),
             pltpu.VMEM((SLOTS, 2, FROWS, 128), F32),
@@ -493,10 +496,13 @@
             pltpu.VMEM((SLOTS, VROWS, 128), F32),
             pltpu.VMEM((SLOTS, VROWS, 128), F32),
             pltpu.VMEM((3, FROWS, 128), F32),
-            dma((2,)),
+            dma((4, 2)),
+            dma,
+            dma((CHUNKS,)),
+            dma((CHUNKS,)),
+            dma((CHUNKS, 2)),
             dma((MEM,)),
-            dma((MEM,)),
-            dma((MEM,)),
+            dma((CHUNKS, 2)),
             dma((MEM,)),
             dma((8,)),
             dma((8,)),
@@ -508,7 +514,7 @@
         ],
         compiler_params=pltpu.CompilerParams(collective_id=0, has_side_effects=True),
         name="smooth",
-    )(fields)
+    )(potential, source, side_faces, end_faces)
 
 
 def prolong_kernel(e, p, corrected, correction, w_fine, w_plain):
@@ -589,8 +595,7 @@
 
 
 def per_device(potential, source, side_faces, end_faces):
-    fields = restrict(potential, source, side_faces, end_faces)
-    e = smooth(fields)
+    e = smooth(potential, source, side_faces, end_faces)
     return prolong(e, potential)
 
 

time: 59.3 us -> 50.5 us (0.85)
  Pallas kernels: 57.9 us -> 49 us
    pallas_call x1 -> x0, Pallas kernels: 5.86 us -> none  [restrict(): pl.pallas_call(restrict_kernel, out_shape=jax.ShapeDtypeStruct((3, MEM, 2...]
    pallas_call x1, Pallas kernels: 46.1 us -> 43 us  [smooth(): pl.pallas_call(smooth_kernel, out_shape=jax.ShapeDtypeStruct((2, MEM, 2,...]
where the time goes in v3:
time: 50.5 us; the launch traced here: 49.7 us
  Pallas kernels  49 us (97%)
  between operations  0.64 us (1%)
    pallas_call x1, Pallas kernels, smooth(): pl.pallas_call(smooth_kernel, out_shape=jax.ShapeDtypeStruct((2, MEM, 2,...  43 us
    pallas_call x1, Pallas kernels, prolong(): pl.pallas_call(prolong_kernel, grid=(CHUNKS,), out_shape=(jax.ShapeDtypeS...  5.97 us

profile of v3, /device:TPU:129, one launch (start us, length us, event | category | flops | bytes accessed | tf_op | source)
XLA Modules:
  0.0 49.7 jit_solution(12494390104864476095)
XLA Ops:
  0.6 43.0 %smooth.1.e = f32[2,8,2,32,128]{4,3,2,1,0:T(8,128)} custom-call(f32[2,512,512]{2,1,0:T(8,128)} %p.1, f32[2,512,512]{2,1,0:T(8,128)} %s_hbm.1, f32[1,4,256]{2,1,0:T(4,128)} %side.1, f32[2,256,256]{2,1,0:T(8,128)} %end_hbm.1), custom_call_target="tpu_custom_call" | custom-call | tf_op jit(solution)/shard_map/smooth/pallas_call | solution.py:478
  43.7 6.0 %prolong.1 = (f32[2,512,512]{2,1,0:T(8,128)}, f32[1,256,256]{2,1,0:T(8,128)}) custom-call(f32[2,8,2,32,128]{4,3,2,1,0:T(8,128)} %smooth.1.e, f32[2,512,512]{2,1,0:T(8,128)} %p.1), custom_call_target="tpu_custom_call" | custom-call | tf_op jit(solution)/shard_map/prolong/pallas_call | solution.py:577

commit v4 on v3

--- a/solution.py
+++ b/solution.py
@@ -50,10 +50,10 @@
 
 
 def smooth_kernel(
-    p_hbm, s_hbm, side, end_hbm, e_out,
-    pb, sb, eb, w_rc, w_lr, w_perm, fields, partner, summed, fb, xb, vr, vk, vk2, scales,
+    p_hbm, s_hbm, side, end_hbm, e_out, pb,
+    sb, eb, w_rc, w_lr, w_perm, fields, partner, summed, fb, xb, vr, vk, vk2, scales,
     in_sems, end_sem, p_send, p_recv, f_send, f_recv, x_send, x_recv, h_send, h_recv, b_send, b_recv,
-    e_send, e_recv, e_local,
+    e_send, e_recv,
 ):
     groups = lax.axis_size("grp")
     g = lax.axis_index("grp")
@@ -306,7 +306,9 @@
         )
 
     def receive(n, carry):
-        k = lax.rem(m // blocks * blocks + 2 * MEM - blocks * (1 + n // blocks) + lax.rem(n, blocks), MEM)
+        back = jnp.where(n == 0, 1, jnp.where(n < 3, 2, jnp.where(n < 5, 3, jnp.where(n < 7, 0, 1))))
+        second = jnp.where(n < 7, jnp.where(n < 5, lax.rem(n, 2) == 1, n == 6), True)
+        k = lax.rem(m // blocks + CHUNKS - back, CHUNKS) * blocks + jnp.where(second, 1, 0)
 
         @pl.when(m != k)
         def _():
@@ -394,7 +396,7 @@
         for i in range(MEM):
             tm = lax.rem(m + i, MEM)
             if i == 0:
-                pltpu.make_async_copy(values.at[HALO + m, v_rows], e_out.at[0, m, colour], e_local.at[0, colour]).start()
+                e_out[0, m, colour] = values[HALO + m, HALO + 8 : HALO + 8 + ROWS, :]
             else:
                 copy = remote(
                     values.at[HALO + tm, v_rows], e_out.at[0, m, colour],
@@ -414,7 +416,7 @@
 
                 @pl.when(jnp.logical_not(wraps))
                 def _():
-                    pltpu.make_async_copy(values.at[plane, v_rows], e_out.at[1, m, colour], e_local.at[1, colour]).start()
+                    e_out[1, m, colour] = values[plane, HALO + 8 : HALO + 8 + ROWS, :]
             else:
                 sends = jnp.logical_not(jnp.logical_and(wraps, g == 0))
             e_copies.append((copy, sends))
@@ -438,12 +440,6 @@
         def _():
             h_copies[o].wait_send()
     for colour, values in ((0, vr), (1, vk2)):
-        pltpu.make_async_copy(values.at[HALO, v_rows], e_out.at[0, m, colour], e_local.at[0, colour]).wait()
-
-        @pl.when(m != MEM - 1)
-        def _():
-            pltpu.make_async_copy(values.at[HALO, v_rows], e_out.at[1, m, colour], e_local.at[1, colour]).wait()
-
         for q in range(MEM):
             def wait_for(part):
                 remote(
@@ -474,14 +470,13 @@
 
 def smooth(potential, source, side_faces, end_faces):
     dma = pltpu.SemaphoreType.DMA
-    anyspace = pl.BlockSpec(memory_space=pl.ANY)
+    anyspace = pl.BlockSpec(memory_space=pltpu.HBM)
     return pl.pallas_call(
         smooth_kernel,
-        out_shape=jax.ShapeDtypeStruct((2, MEM, 2, ROWS, 128), F32),
+        out_shape=(pltpu.VMEM((2, MEM, 2, ROWS, 128), F32), pltpu.VMEM((2, 4, NF + 16, 128), F32)),
         in_specs=[anyspace, anyspace, pl.BlockSpec(memory_space=pltpu.VMEM), anyspace],
-        out_specs=anyspace,
+        out_specs=(pl.BlockSpec(memory_space=pltpu.VMEM), pl.BlockSpec(memory_space=pltpu.VMEM)),
         scratch_shapes=[
-            pltpu.VMEM((2, 4, NF + 16, 128), F32),
             pltpu.VMEM((2, 4, NF + 16, 128), F32),
             pltpu.VMEM((NC, NC), F32),
             pltpu.VMEM((NF, NC), BF16),
@@ -510,93 +505,102 @@
             dma((8,)),
             dma((2, 2, MEM)),
             dma((2, 2, MEM)),
-            dma((2, 2)),
         ],
         compiler_params=pltpu.CompilerParams(collective_id=0, has_side_effects=True),
         name="smooth",
     )(potential, source, side_faces, end_faces)
 
 
-def prolong_kernel(e, p, corrected, correction, w_fine, w_plain):
+def prolong_kernel(e, p, corrected, correction, w_fine, w_plain, fine, coarse, sems):
     groups = lax.axis_size("grp")
     device = lax.axis_index("grp") * MEM + lax.axis_index("mem")
     is_last = device == groups * MEM - 1
-    c = pl.program_id(0)
     blocks = CROWS // ROWS
 
-    @pl.when(c == 0)
-    def _():
-        column = coarse_column((NC, NF), 0)
-        fine = iota((NC, NF), 1)
-        step = fine - 2 * column
-        whole = jnp.logical_or(step == 0, jnp.logical_and(step == 1, column == NC - 1))
-        half = jnp.logical_or(step == 1, step == -1)
-        w_fine[...] = jnp.where(whole, 1.0, jnp.where(half, 0.5, 0.0)).astype(BF16)
-        w_plain[...] = jnp.where(
-            iota((NC, NC), 1) == coarse_column((NC, NC), 0), 1.0, 0.0
-        ).astype(BF16)
-
-    def by_column(part, shift, red, black):
-        row = iota(red.shape, 0)
-        even = lax.rem(row + shift + device, 2) == 0
+    column = coarse_column((NC, NF), 0)
+    step = iota((NC, NF), 1) - 2 * column
+    whole = jnp.logical_or(step == 0, jnp.logical_and(step == 1, column == NC - 1))
+    half = jnp.logical_or(step == 1, step == -1)
+    w_fine[...] = jnp.where(whole, 1.0, jnp.where(half, 0.5, 0.0)).astype(BF16)
+    w_plain[...] = jnp.where(iota((NC, NC), 1) == coarse_column((NC, NC), 0), 1.0, 0.0).astype(BF16)
+
+    def by_column(part, red, black):
+        even = lax.rem(iota(red.shape, 0) + part + device, 2) == 0
         return jnp.concatenate([jnp.where(even, red, black), jnp.where(even, black, red)], axis=1)
 
-    def rows_of(part):
-        here = [by_column(part, part, e[part, c * blocks + b, 0], e[part, c * blocks + b, 1]) for b in range(blocks)]
-        q = jnp.minimum(c * blocks + blocks, MEM - 1)
-        after = by_column(part, part, e[part, q, 0, 0:8, :], e[part, q, 1, 0:8, :])
+    def rows_of(part, c):
+        here = [by_column(part, e[part, c * blocks + b, 0], e[part, c * blocks + b, 1]) for b in range(blocks)]
+        q = min(c * blocks + blocks, MEM - 1)
+        after = by_column(part, e[part, q, 0, 0:8, :], e[part, q, 1, 0:8, :])
         return jnp.concatenate(here, axis=0), after
-
-    here, after = rows_of(0)
-    here_up, after_up = rows_of(1)
-    at_bottom = c == CHUNKS - 1
 
     r = iota((FINE, CROWS), 0)
     k = iota((FINE, CROWS), 1)
-    last_row = jnp.logical_and(jnp.logical_and(r == FINE - 1, k == CROWS - 1), at_bottom)
-    take = jnp.where(
-        jnp.logical_or(r == 2 * k, last_row), 1.0,
-        jnp.where(jnp.logical_or(r == 2 * k + 1, r == 2 * k - 1), 0.5, 0.0),
-    ).astype(BF16)
-
-    def down(x, next_rows):
-        parts = jnp.concatenate(split3(x), axis=1)
-        out = jnp.dot(take, parts, preferred_element_type=F32)
-        out = out[:, :NC] + (out[:, NC : 2 * NC] + out[:, 2 * NC :])
-        carry = jnp.where(at_bottom, 0.0, 0.5 * next_rows[0:1, :])
-        return out + jnp.where(iota((FINE, NC), 0) == FINE - 1, carry, 0.0)
-
-    above = jnp.where(is_last, here, 0.5 * (here + here_up))
-    above_after = jnp.where(is_last, after, 0.5 * (after + after_up))
-    corrected[0] = p[0] + dot_exact(down(here, after), w_fine[...])
-    corrected[1] = p[1] + dot_exact(down(above, above_after), w_fine[...])
-    correction[0] = dot_exact(here, w_plain[...])
+    halves = jnp.logical_or(r == 2 * k + 1, r == 2 * k - 1)
+    copies = []
+    for c in range(CHUNKS):
+        at_bottom = c == CHUNKS - 1
+        wholes = r == 2 * k
+        if at_bottom:
+            wholes = jnp.logical_or(wholes, jnp.logical_and(r == FINE - 1, k == CROWS - 1))
+        take = jnp.where(wholes, 1.0, jnp.where(halves, 0.5, 0.0)).astype(BF16)
+
+        def down(x, next_rows):
+            parts = jnp.concatenate(split3(x), axis=1)
+            out = jnp.dot(take, parts, preferred_element_type=F32)
+            out = out[:, :NC] + (out[:, NC : 2 * NC] + out[:, 2 * NC :])
+            if at_bottom:
+                return out
+            return out + jnp.where(iota((FINE, NC), 0) == FINE - 1, 0.5 * next_rows[0:1, :], 0.0)
+
+        here, after = rows_of(0, c)
+        here_up, after_up = rows_of(1, c)
+        above = jnp.where(is_last, here, 0.5 * (here + here_up))
+        above_after = jnp.where(is_last, after, 0.5 * (after + after_up))
+        rows = pl.ds(FINE * c, FINE)
+        for plane, (x, next_rows) in enumerate(((here, after), (above, above_after))):
+            refined = dot_exact(down(x, next_rows), w_fine[...])
+            for t in range(4):
+                lanes = slice(128 * t, 128 * t + 128)
+                fine[plane, rows, lanes] = p[plane, t, pl.ds(8 + FINE * c, FINE), :] + refined[:, lanes]
+            copy = pltpu.make_async_copy(fine.at[plane, rows], corrected.at[plane, rows], sems.at[c, plane])
+            copy.start()
+            copies.append(copy)
+        rows = pl.ds(CROWS * c, CROWS)
+        coarse[rows, :] = dot_exact(here, w_plain[...])
+        copy = pltpu.make_async_copy(coarse.at[rows], correction.at[0, rows], sems.at[c, 2])
+        copy.start()
+        copies.append(copy)
+    for copy in copies:
+        copy.wait()
 
 
 def prolong(e, potential):
+    vmem = pl.BlockSpec(memory_space=pltpu.VMEM)
+    anyspace = pl.BlockSpec(memory_space=pl.ANY)
     return pl.pallas_call(
         prolong_kernel,
-        grid=(CHUNKS,),
         out_shape=(
             jax.ShapeDtypeStruct((2, NF, NF), F32),
             jax.ShapeDtypeStruct((1, NC, NC), F32),
         ),
-        in_specs=[
-            pl.BlockSpec((2, MEM, 2, ROWS, 128), lambda c: (0, 0, 0, 0, 0)),
-            pl.BlockSpec((2, FINE, NF), lambda c: (0, c, 0)),
+        in_specs=[vmem, vmem],
+        out_specs=(anyspace, anyspace),
+        scratch_shapes=[
+            pltpu.VMEM((NC, NF), BF16),
+            pltpu.VMEM((NC, NC), BF16),
+            pltpu.VMEM((2, NF, NF), F32),
+            pltpu.VMEM((NC, NC), F32),
+            pltpu.SemaphoreType.DMA((CHUNKS, 3)),
         ],
-        out_specs=(
-            pl.BlockSpec((2, FINE, NF), lambda c: (0, c, 0)),
-            pl.BlockSpec((1, CROWS, NC), lambda c: (0, c, 0)),
-        ),
-        scratch_shapes=[pltpu.VMEM((NC, NF), BF16), pltpu.VMEM((NC, NC), BF16)],
+        compiler_params=pltpu.CompilerParams(vmem_limit_bytes=24 * 2**20),
         name="prolong",
-    )(e, potential)
+    )(*(pltpu.with_memory_space_constraint(x, pltpu.VMEM) for x in (e, potential)))
 
 
 def per_device(potential, source, side_faces, end_faces):
-    e = smooth(potential, source, side_faces, end_faces)
-    return prolong(e, potential)
+    e, kept = smooth(potential, source, side_faces, end_faces)
+    return prolong(e, kept)
 
 
 def solution(mesh):

time: 50.5 us -> 48.4 us (0.958); the launches traced: 49.7 us -> 48.3 us
  Pallas kernels: 49 us -> 47.7 us
    pallas_call x2, Pallas kernels: 49 us -> 47.7 us  [the longest x1 44.1 us: smooth(): pl.pallas_call(smooth_kernel, out_shape=(pltpu.VMEM((2, MEM, 2, ROWS, 128...]
where the time goes in v4:
time: 48.4 us; the launch traced here: 48.3 us
  Pallas kernels  47.7 us (99%)
  between operations  0.64 us (1%)
    pallas_call x1, Pallas kernels, smooth(): pl.pallas_call(smooth_kernel, out_shape=(pltpu.VMEM((2, MEM, 2, ROWS, 128...  44.1 us
    pallas_call x1, Pallas kernels, prolong(): pl.pallas_call(prolong_kernel, out_shape=(jax.ShapeDtypeStruct((2, NF, NF...  3.55 us

profile of v4, /device:TPU:129, one launch (start us, length us, event | category | flops | bytes accessed | tf_op | source)
XLA Modules:
  0.0 48.3 jit_solution(4618692799960070350)
XLA Ops:
  0.6 44.1 %smooth.1 = (f32[2,8,2,32,128]{4,3,2,1,0:T(8,128)S(1)}, f32[2,4,528,128]{3,2,1,0:T(8,128)S(1)}) custom-call(f32[2,512,512]{2,1,0:T(8,128)} %p_hbm.1, f32[2,512,512]{2,1,0:T(8,128)} %s_hbm.1, f32[1,4,256]{2,1,0:T(4,128)} %side.1, f32[2,256,256]{2,1,0:T(8,128)} %end_hbm.1), custom_call_target="tpu_custom_call" | custom-call | tf_op jit(solution)/shard_map/smooth/pallas_call | solution.py:474
  44.8 3.5 %prolong.1 = (f32[2,512,512]{2,1,0:T(8,128)}, f32[1,256,256]{2,1,0:T(8,128)}) custom-call(f32[2,8,2,32,128]{4,3,2,1,0:T(8,128)S(1)} %get-tuple-element.4.e, f32[2,4,528,128]{3,2,1,0:T(8,128)S(1)} %get-tuple-element.5.p), custom_call_target="tpu_custom_call" | custom-call | tf_op jit(solution)/shard_map/prolong/pallas_call | solution.py:581

commit v5 on v4

--- a/solution.py
+++ b/solution.py
@@ -50,7 +50,7 @@
 
 
 def smooth_kernel(
-    p_hbm, s_hbm, side, end_hbm, e_out, pb,
+    p_hbm, s_hbm, side, end_hbm, e_out, pb, w_fine, w_plain,
     sb, eb, w_rc, w_lr, w_perm, fields, partner, summed, fb, xb, vr, vk, vk2, scales,
     in_sems, end_sem, p_send, p_recv, f_send, f_recv, x_send, x_recv, h_send, h_recv, b_send, b_recv,
     e_send, e_recv,
@@ -237,9 +237,9 @@
     def _():
         end_copy.wait()
 
+    order = [lax.rem(m // blocks + k, CHUNKS) for k in (1, 3, 0, 2)]
     partners = []
-    for i in range(CHUNKS):
-        c = lax.rem(m // blocks + 1 + i, CHUNKS)
+    for i, c in enumerate(order):
         restrict(c)
 
         @pl.when(at_end)
@@ -251,8 +251,8 @@
             pl.semaphore_wait(barrier, count)
         partners.append(send_fields(i, c))
         if i > 0:
-            send_sums(i - 1, lax.rem(m // blocks + i, CHUNKS), partners[i - 1])
-    send_sums(CHUNKS - 1, m // blocks, partners[-1])
+            send_sums(i - 1, order[i - 1], partners[i - 1])
+    send_sums(CHUNKS - 1, order[-1], partners[-1])
 
     def inside(dg, dm):
         ok = None
@@ -306,9 +306,8 @@
         )
 
     def receive(n, carry):
-        back = jnp.where(n == 0, 1, jnp.where(n < 3, 2, jnp.where(n < 5, 3, jnp.where(n < 7, 0, 1))))
-        second = jnp.where(n < 7, jnp.where(n < 5, lax.rem(n, 2) == 1, n == 6), True)
-        k = lax.rem(m // blocks + CHUNKS - back, CHUNKS) * blocks + jnp.where(second, 1, 0)
+        offset = jnp.where(n < 4, n - 1, jnp.where(n == 4, -2, n - 2))
+        k = lax.rem(m // blocks * blocks + offset + MEM, MEM)
 
         @pl.when(m != k)
         def _():
@@ -345,6 +344,13 @@
         )
 
     lax.fori_loop(0, MEM, receive, 0)
+    column = coarse_column((NC, NF), 0)
+    step = iota((NC, NF), 1) - 2 * column
+    whole = jnp.logical_or(step == 0, jnp.logical_and(step == 1, column == NC - 1))
+    half = jnp.abs(step) == 1
+    w_fine[...] = jnp.where(whole, 1.0, jnp.where(half, 0.5, 0.0)).astype(BF16)
+    w_plain[...] = jnp.where(iota((NC, NC), 1) == coarse_column((NC, NC), 0), 1.0, 0.0).astype(BF16)
+
     h_copies = [forcing_copy(o, dg, dm) for o, (dg, dm) in enumerate(DIRECTIONS)]
     arrive(h_copies)
 
@@ -473,9 +479,14 @@
     anyspace = pl.BlockSpec(memory_space=pltpu.HBM)
     return pl.pallas_call(
         smooth_kernel,
-        out_shape=(pltpu.VMEM((2, MEM, 2, ROWS, 128), F32), pltpu.VMEM((2, 4, NF + 16, 128), F32)),
+        out_shape=(
+            pltpu.VMEM((2, MEM, 2, ROWS, 128), F32),
+            pltpu.VMEM((2, 4, NF + 16, 128), F32),
+            pltpu.VMEM((NC, NF), BF16),
+            pltpu.VMEM((NC, NC), BF16),
+        ),
         in_specs=[anyspace, anyspace, pl.BlockSpec(memory_space=pltpu.VMEM), anyspace],
-        out_specs=(pl.BlockSpec(memory_space=pltpu.VMEM), pl.BlockSpec(memory_space=pltpu.VMEM)),
+        out_specs=(pl.BlockSpec(memory_space=pltpu.VMEM),) * 4,
         scratch_shapes=[
             pltpu.VMEM((2, 4, NF + 16, 128), F32),
             pltpu.VMEM((NC, NC), F32),
@@ -511,71 +522,57 @@
     )(potential, source, side_faces, end_faces)
 
 
-def prolong_kernel(e, p, corrected, correction, w_fine, w_plain, fine, coarse, sems):
+def prolong_kernel(e, p, w_fine, w_plain, corrected, correction, wide, fine, coarse, sems, coarse_sems):
     groups = lax.axis_size("grp")
     device = lax.axis_index("grp") * MEM + lax.axis_index("mem")
     is_last = device == groups * MEM - 1
     blocks = CROWS // ROWS
 
-    column = coarse_column((NC, NF), 0)
-    step = iota((NC, NF), 1) - 2 * column
-    whole = jnp.logical_or(step == 0, jnp.logical_and(step == 1, column == NC - 1))
-    half = jnp.logical_or(step == 1, step == -1)
-    w_fine[...] = jnp.where(whole, 1.0, jnp.where(half, 0.5, 0.0)).astype(BF16)
-    w_plain[...] = jnp.where(iota((NC, NC), 1) == coarse_column((NC, NC), 0), 1.0, 0.0).astype(BF16)
-
     def by_column(part, red, black):
         even = lax.rem(iota(red.shape, 0) + part + device, 2) == 0
         return jnp.concatenate([jnp.where(even, red, black), jnp.where(even, black, red)], axis=1)
 
     def rows_of(part, c):
         here = [by_column(part, e[part, c * blocks + b, 0], e[part, c * blocks + b, 1]) for b in range(blocks)]
-        q = min(c * blocks + blocks, MEM - 1)
-        after = by_column(part, e[part, q, 0, 0:8, :], e[part, q, 1, 0:8, :])
-        return jnp.concatenate(here, axis=0), after
-
-    r = iota((FINE, CROWS), 0)
-    k = iota((FINE, CROWS), 1)
-    halves = jnp.logical_or(r == 2 * k + 1, r == 2 * k - 1)
+        if c == CHUNKS - 1:
+            after = jnp.broadcast_to(here[-1][ROWS - 1 :, :], (8, NC))
+        else:
+            q = (c + 1) * blocks
+            after = by_column(part, e[part, q, 0, 0:8, :], e[part, q, 1, 0:8, :])
+        return jnp.concatenate(here + [after], axis=0)
+
     copies = []
     for c in range(CHUNKS):
-        at_bottom = c == CHUNKS - 1
-        wholes = r == 2 * k
-        if at_bottom:
-            wholes = jnp.logical_or(wholes, jnp.logical_and(r == FINE - 1, k == CROWS - 1))
-        take = jnp.where(wholes, 1.0, jnp.where(halves, 0.5, 0.0)).astype(BF16)
-
-        def down(x, next_rows):
-            parts = jnp.concatenate(split3(x), axis=1)
-            out = jnp.dot(take, parts, preferred_element_type=F32)
-            out = out[:, :NC] + (out[:, NC : 2 * NC] + out[:, 2 * NC :])
-            if at_bottom:
-                return out
-            return out + jnp.where(iota((FINE, NC), 0) == FINE - 1, 0.5 * next_rows[0:1, :], 0.0)
-
-        here, after = rows_of(0, c)
-        here_up, after_up = rows_of(1, c)
-        above = jnp.where(is_last, here, 0.5 * (here + here_up))
-        above_after = jnp.where(is_last, after, 0.5 * (after + after_up))
-        rows = pl.ds(FINE * c, FINE)
-        for plane, (x, next_rows) in enumerate(((here, after), (above, above_after))):
-            refined = dot_exact(down(x, next_rows), w_fine[...])
+        rows = rows_of(0, c)
+        above = jnp.where(is_last, rows, 0.5 * (rows + rows_of(1, c)))
+        out_rows = pl.ds(FINE * c, FINE)
+        for plane, x in enumerate((rows, above)):
+            refined = dot_exact(x, w_fine[...])
             for t in range(4):
-                lanes = slice(128 * t, 128 * t + 128)
-                fine[plane, rows, lanes] = p[plane, t, pl.ds(8 + FINE * c, FINE), :] + refined[:, lanes]
-            copy = pltpu.make_async_copy(fine.at[plane, rows], corrected.at[plane, rows], sems.at[c, plane])
-            copy.start()
-            copies.append(copy)
-        rows = pl.ds(CROWS * c, CROWS)
-        coarse[rows, :] = dot_exact(here, w_plain[...])
-        copy = pltpu.make_async_copy(coarse.at[rows], correction.at[0, rows], sems.at[c, 2])
+                wide[plane, t] = refined[:, 128 * t : 128 * t + 128]
+                here, after = wide[plane, t, 0:CROWS, :], wide[plane, t, 1 : CROWS + 1, :]
+                even, odd = pl.ds(FINE * c, CROWS, stride=2), pl.ds(FINE * c + 1, CROWS, stride=2)
+                p_even = p[plane, t, pl.ds(8 + FINE * c, CROWS, stride=2), :]
+                p_odd = p[plane, t, pl.ds(9 + FINE * c, CROWS, stride=2), :]
+                fine[plane, t, even, :] = p_even + here
+                fine[plane, t, odd, :] = p_odd + 0.5 * (here + after)
+                copy = pltpu.make_async_copy(
+                    fine.at[plane, t, out_rows],
+                    corrected.at[plane, out_rows, pl.ds(128 * t, 128)],
+                    sems.at[c, plane, t],
+                )
+                copy.start()
+                copies.append(copy)
+        out_rows = pl.ds(CROWS * c, CROWS)
+        coarse[out_rows, :] = dot_exact(rows[:CROWS], w_plain[...])
+        copy = pltpu.make_async_copy(coarse.at[out_rows], correction.at[0, out_rows], coarse_sems.at[c])
         copy.start()
         copies.append(copy)
     for copy in copies:
         copy.wait()
 
 
-def prolong(e, potential):
+def prolong(*values):
     vmem = pl.BlockSpec(memory_space=pltpu.VMEM)
     anyspace = pl.BlockSpec(memory_space=pl.ANY)
     return pl.pallas_call(
@@ -584,23 +581,22 @@
             jax.ShapeDtypeStruct((2, NF, NF), F32),
             jax.ShapeDtypeStruct((1, NC, NC), F32),
         ),
-        in_specs=[vmem, vmem],
+        in_specs=[vmem] * 4,
         out_specs=(anyspace, anyspace),
         scratch_shapes=[
-            pltpu.VMEM((NC, NF), BF16),
-            pltpu.VMEM((NC, NC), BF16),
-            pltpu.VMEM((2, NF, NF), F32),
+            pltpu.VMEM((2, 4, CROWS + 8, 128), F32),
+            pltpu.VMEM((2, 4, NF, 128), F32),
             pltpu.VMEM((NC, NC), F32),
-            pltpu.SemaphoreType.DMA((CHUNKS, 3)),
+            pltpu.SemaphoreType.DMA((CHUNKS, 2, 4)),
+            pltpu.SemaphoreType.DMA((CHUNKS,)),
         ],
         compiler_params=pltpu.CompilerParams(vmem_limit_bytes=24 * 2**20),
         name="prolong",
-    )(*(pltpu.with_memory_space_constraint(x, pltpu.VMEM) for x in (e, potential)))
+    )(*(pltpu.with_memory_space_constraint(x, pltpu.VMEM) for x in values))
 
 
 def per_device(potential, source, side_faces, end_faces):
-    e, kept = smooth(potential, source, side_faces, end_faces)
-    return prolong(e, kept)
+    return prolong(*smooth(potential, source, side_faces, end_faces))
 
 
 def solution(mesh):

time: 48.4 us -> 46 us (0.950)
  Pallas kernels: 47.7 us -> 45.2 us
    pallas_call x1, Pallas kernels: 3.55 us -> 2.01 us  [prolong(): pl.pallas_call(prolong_kernel, out_shape=(jax.ShapeDtypeStruct((2, NF, NF...]
    pallas_call x1, Pallas kernels: 44.1 us -> 43.2 us  [smooth(): pl.pallas_call(smooth_kernel, out_shape=(pltpu.VMEM((2, MEM, 2, ROWS, 128...]
where the time goes in v5:
time: 46 us; the launch traced here: 45.8 us
  Pallas kernels  45.2 us (98%)
  between operations  0.64 us (1%)
    pallas_call x1, Pallas kernels, smooth(): pl.pallas_call(smooth_kernel, out_shape=(pltpu.VMEM((2, MEM, 2, ROWS, 128...  43.2 us
    pallas_call x1, Pallas kernels, prolong(): pl.pallas_call(prolong_kernel, out_shape=(jax.ShapeDtypeStruct((2, NF, NF...  2.01 us

profile of v5, /device:TPU:129, one launch (start us, length us, event | category | flops | bytes accessed | tf_op | source)
XLA Modules:
  0.0 45.8 jit_solution(8767429880803952573)
XLA Ops:
  0.6 43.2 %smooth.1 = (f32[2,8,2,32,128]{4,3,2,1,0:T(8,128)S(1)}, f32[2,4,528,128]{3,2,1,0:T(8,128)S(1)}, bf16[256,512]{1,0:T(8,128)(2,1)S(1)}, bf16[256,256]{1,0:T(8,128)(2,1)S(1)}) custom-call(f32[2,512,512]{2,1,0:T(8,128)} %p_hbm.1, f32[2,512,512]{2,1,0:T(8,128)} %s_hbm.1, f32[1,4,256]{2,1,0:T(4,128)} %side.1, f32[2,256,256]{2,1,0:T(8,128)} %end_hbm.1), custom_call_target="tpu_custom_call" | custom-call | tf_op jit(solution)/shard_map/smooth/pallas_call | solution.py:480
  43.8 2.0 %prolong.1 = (f32[2,512,512]{2,1,0:T(8,128)}, f32[1,256,256]{2,1,0:T(8,128)}) custom-call(f32[2,8,2,32,128]{4,3,2,1,0:T(8,128)S(1)} %get-tuple-element.6.e, f32[2,4,528,128]{3,2,1,0:T(8,128)S(1)} %get-tuple-element.7.p, bf16[256,512]{1,0:T(8,128)(2,1)S(1)} %get-tuple-element.8.w_fine, bf16[256,256]{1,0:T(8,128)(2,1)S(1)} %get-tuple-element.9.w_plain), custom_call_target="tpu_custom_call" | custom-call | tf_op jit(solution)/shard_map/prolong/pallas_call | solution.py:578

commit v6 on v5

--- a/solution.py
+++ b/solution.py
@@ -125,9 +125,6 @@
     front = dot_exact(jnp.broadcast_to(side[0, 0:1, :], (8, NC)), w_perm[...])[0:1]
     back = dot_exact(jnp.broadcast_to(side[0, 1:2, :], (8, NC)), w_perm[...])[0:1]
     own_weight = jnp.where(is_first, 0.25, 0.5)
-    for copy in in_copies:
-        copy.wait()
-
     blocks = CROWS // ROWS
 
     def by_colour(value, shift):
@@ -135,10 +132,13 @@
         left, right = value[:, :128], value[:, 128:]
         return jnp.where(even, left, right), jnp.where(even, right, left)
 
-    def restrict(c):
+    def restrict(c, first):
         lists = [[], [], [], [], []]
         row = CROWS * c + iota((CROWS, 128), 0)
         for t in range(4):
+            if first:
+                for copy in in_copies[2 * t : 2 * t + 2]:
+                    copy.wait()
 
             def load(ref, plane, shift):
                 return ref[plane, t, pl.ds(8 + FINE * c + shift, CROWS, stride=2), :]
@@ -198,25 +198,29 @@
         def _():
             copy.start()
 
+    def send_x(i, c, colour):
+        for b in range(blocks):
+            q = c * blocks + b
+            home = jnp.logical_and(x_home, q == m)
+            send_if(
+                jnp.logical_and(x_valid, jnp.logical_not(home)),
+                remote(
+                    fields.at[x_field, q, colour], xb.at[x_plane, colour],
+                    x_send.at[i, b, colour], x_recv.at[x_plane, colour], x_group, q,
+                ),
+            )
+
+            @pl.when(home)
+            def _():
+                xb[x_plane, colour] = fields[x_field, q, colour]
+
     def send_fields(i, c):
         part = pl.ds(c * blocks, blocks)
         copy = remote(
             fields.at[1 + odd, part], partner.at[part], p_send.at[i], p_recv.at[i], g, m + 1 - 2 * odd
         )
         copy.start()
-        for b in range(blocks):
-            q = c * blocks + b
-            home = jnp.logical_and(x_home, q == m)
-            send_if(
-                jnp.logical_and(x_valid, jnp.logical_not(home)),
-                remote(
-                    fields.at[x_field, q], xb.at[x_plane], x_send.at[i, b], x_recv.at[x_plane], x_group, q
-                ),
-            )
-
-            @pl.when(home)
-            def _():
-                xb[x_plane] = fields[x_field, q]
+        send_x(i, c, 0)
         return copy
 
     def send_sums(i, c, to_partner):
@@ -224,14 +228,23 @@
         for b in range(blocks):
             q = c * blocks + b
             summed[q] = fields[0, q] + partner[q]
-            send_if(
-                q != m,
-                remote(summed.at[q], fb.at[HALO + m, :, own_rows], f_send.at[i, b], f_recv.at[m], g, q),
-            )
 
             @pl.when(q == m)
             def _():
                 fb[HALO + m, :, HALO : HALO + ROWS, :] = summed[q]
+
+        for colour in (0, 1):
+            if colour == 1:
+                send_x(i, c, 1)
+            for b in range(blocks):
+                q = c * blocks + b
+                send_if(
+                    q != m,
+                    remote(
+                        summed.at[q, colour], fb.at[HALO + m, colour, own_rows],
+                        f_send.at[i, b, colour], f_recv.at[m, colour], g, q,
+                    ),
+                )
 
     @pl.when(at_end)
     def _():
@@ -240,7 +253,7 @@
     order = [lax.rem(m // blocks + k, CHUNKS) for k in (1, 3, 0, 2)]
     partners = []
     for i, c in enumerate(order):
-        restrict(c)
+        restrict(c, i == 0)
 
         @pl.when(at_end)
         def _():
@@ -295,23 +308,29 @@
             return pl.ds(HALO + MEM - depth, depth), pl.ds(HALO - depth, depth)
         return pl.ds(HALO, MEM), pl.ds(HALO, MEM)
 
-    def forcing_copy(o, dg, dm, k=None):
+    def forcing_copy(o, dg, dm, k=None, colour=0):
         src_rows, dst_rows = row_parts(dm, HALO)
         if k is None:
             src, dst = plane_parts(dg, HALO - 1 - abs(dm))
+            colour = slice(None)
         else:
             src, dst = HALO + k, HALO + k - MEM * dg
         return remote(
-            fb.at[src, :, src_rows], fb.at[dst, :, dst_rows], h_send.at[o], h_recv.at[o], g + dg, m + dm
+            fb.at[src, colour, src_rows], fb.at[dst, colour, dst_rows], h_send.at[o], h_recv.at[o], g + dg, m + dm
         )
 
     def receive(n, carry):
-        offset = jnp.where(n < 4, n - 1, jnp.where(n == 4, -2, n - 2))
+        colour = lax.rem(n // 4, 2)
+        item = n // 8 * 4 + lax.rem(n, 4)
+        offset = jnp.where(item < 4, item - 1, jnp.where(item == 4, -2, item - 2))
         k = lax.rem(m // blocks * blocks + offset + MEM, MEM)
 
         @pl.when(m != k)
         def _():
-            remote(summed.at[0], fb.at[HALO + k, :, own_rows], f_send.at[0, 0], f_recv.at[k], g, k).wait_recv()
+            remote(
+                summed.at[0, 0], fb.at[HALO + k, colour, own_rows],
+                f_send.at[0, 0, 0], f_recv.at[k, colour], g, k,
+            ).wait_recv()
 
         arrives = jnp.logical_not(jnp.logical_and(x_home, x_plane == k))
         arrives = jnp.logical_and(arrives, jnp.logical_or(k > 0, g > 0))
@@ -319,9 +338,11 @@
 
         @pl.when(arrives)
         def _():
-            remote(fields.at[0, 0], xb.at[k], x_send.at[0, 0], x_recv.at[k], g, k).wait_recv()
-
-        fb[HALO + k, :, HALO : HALO + ROWS, :] = fb[HALO + k, :, HALO : HALO + ROWS, :] + xb[k]
+            remote(
+                fields.at[0, 0, 0], xb.at[k, colour], x_send.at[0, 0, 0], x_recv.at[k, colour], g, k
+            ).wait_recv()
+
+        fb[HALO + k, colour, HALO : HALO + ROWS, :] = fb[HALO + k, colour, HALO : HALO + ROWS, :] + xb[k, colour]
         for o, (dg, dm) in enumerate(DIRECTIONS):
             depth = HALO - 1 - abs(dm)
             needed = inside(dg, dm)
@@ -332,7 +353,7 @@
 
             @pl.when(needed)
             def _():
-                forcing_copy(o, dg, dm, k).start()
+                forcing_copy(o, dg, dm, k, colour).start()
         return carry
 
     def black_copy(o, dg, dm):
@@ -343,7 +364,7 @@
             b_send.at[o], b_recv.at[o], g + dg, m + dm,
         )
 
-    lax.fori_loop(0, MEM, receive, 0)
+    lax.fori_loop(0, 2 * MEM, receive, 0)
     column = coarse_column((NC, NF), 0)
     step = iota((NC, NF), 1) - 2 * column
     whole = jnp.logical_or(step == 0, jnp.logical_and(step == 1, column == NC - 1))
@@ -506,10 +527,10 @@
             dma,
             dma((CHUNKS,)),
             dma((CHUNKS,)),
-            dma((CHUNKS, 2)),
-            dma((MEM,)),
-            dma((CHUNKS, 2)),
-            dma((MEM,)),
+            dma((CHUNKS, 2, 2)),
+            dma((MEM, 2)),
+            dma((CHUNKS, 2, 2)),
+            dma((MEM, 2)),
             dma((8,)),
             dma((8,)),
             dma((8,)),

time: 46 us -> 45.2 us (0.983); the launches traced: 45.8 us -> 44.5 us
  Pallas kernels: 45.2 us -> 43.9 us
    pallas_call x1, Pallas kernels: 43.2 us -> 41.9 us  [smooth(): pl.pallas_call(smooth_kernel, out_shape=(pltpu.VMEM((2, MEM, 2, ROWS, 128...]
where the time goes in v6:
time: 45.2 us; the launch traced here: 44.5 us
  Pallas kernels  43.9 us (97%)
  between operations  0.64 us (1%)
    pallas_call x1, Pallas kernels, smooth(): pl.pallas_call(smooth_kernel, out_shape=(pltpu.VMEM((2, MEM, 2, ROWS, 128...  41.9 us
    pallas_call x1, Pallas kernels, prolong(): pl.pallas_call(prolong_kernel, out_shape=(jax.ShapeDtypeStruct((2, NF, NF...  2 us

profile of v6, /device:TPU:129, one launch (start us, length us, event | category | flops | bytes accessed | tf_op | source)
XLA Modules:
  0.0 44.5 jit_solution(8613612158908261371)
XLA Ops:
  0.6 41.9 %smooth.1 = (f32[2,8,2,32,128]{4,3,2,1,0:T(8,128)S(1)}, f32[2,4,528,128]{3,2,1,0:T(8,128)S(1)}, bf16[256,512]{1,0:T(8,128)(2,1)S(1)}, bf16[256,256]{1,0:T(8,128)(2,1)S(1)}) custom-call(f32[2,512,512]{2,1,0:T(8,128)} %p_hbm.1, f32[2,512,512]{2,1,0:T(8,128)} %s_hbm.1, f32[1,4,256]{2,1,0:T(4,128)} %side.1, f32[2,256,256]{2,1,0:T(8,128)} %end_hbm.1), custom_call_target="tpu_custom_call" | custom-call | tf_op jit(solution)/shard_map/smooth/pallas_call | solution.py:501
  42.5 2.0 %prolong.1 = (f32[2,512,512]{2,1,0:T(8,128)}, f32[1,256,256]{2,1,0:T(8,128)}) custom-call(f32[2,8,2,32,128]{4,3,2,1,0:T(8,128)S(1)} %get-tuple-element.6.e, f32[2,4,528,128]{3,2,1,0:T(8,128)S(1)} %get-tuple-element.7.p, bf16[256,512]{1,0:T(8,128)(2,1)S(1)} %get-tuple-element.8.w_fine, bf16[256,256]{1,0:T(8,128)(2,1)S(1)} %get-tuple-element.9.w_plain), custom_call_target="tpu_custom_call" | custom-call | tf_op jit(solution)/shard_map/prolong/pallas_call | solution.py:599

commit v7 on v6

--- a/solution.py
+++ b/solution.py
@@ -53,7 +53,7 @@
     p_hbm, s_hbm, side, end_hbm, e_out, pb, w_fine, w_plain,
     sb, eb, w_rc, w_lr, w_perm, fields, partner, summed, fb, xb, vr, vk, vk2, scales,
     in_sems, end_sem, p_send, p_recv, f_send, f_recv, x_send, x_recv, h_send, h_recv, b_send, b_recv,
-    e_send, e_recv,
+    e_send, e_recv, fwd_send,
 ):
     groups = lax.axis_size("grp")
     g = lax.axis_index("grp")
@@ -420,17 +420,17 @@
     e_copies = []
 
     def send_back(colour, values):
+        e_out[0, m, colour] = values[HALO + m, HALO + 8 : HALO + 8 + ROWS, :]
+        for i in range(1, MEM):
+            tm = lax.rem(m + i, MEM)
+            copy = remote(
+                values.at[HALO + tm, v_rows], e_out.at[0, m, colour],
+                e_send.at[0, colour, i], e_recv.at[0, colour, m], g, tm,
+            )
+            copy.start()
+            e_copies.append((copy, None))
         for i in range(MEM):
             tm = lax.rem(m + i, MEM)
-            if i == 0:
-                e_out[0, m, colour] = values[HALO + m, HALO + 8 : HALO + 8 + ROWS, :]
-            else:
-                copy = remote(
-                    values.at[HALO + tm, v_rows], e_out.at[0, m, colour],
-                    e_send.at[0, colour, i], e_recv.at[0, colour, m], g, tm,
-                )
-                copy.start()
-                e_copies.append((copy, None))
             wraps = tm == MEM - 1
             plane = HALO + jnp.where(wraps, 0, tm + 1)
             tg = g - jnp.where(wraps, 1, 0)
@@ -445,7 +445,8 @@
                 def _():
                     e_out[1, m, colour] = values[plane, HALO + 8 : HALO + 8 + ROWS, :]
             else:
-                sends = jnp.logical_not(jnp.logical_and(wraps, g == 0))
+                direct = jnp.logical_or(lax.rem(tm, 2) == 1, tm // blocks == m // blocks)
+                sends = jnp.logical_and(direct, jnp.logical_not(jnp.logical_and(wraps, g == 0)))
             e_copies.append((copy, sends))
 
             @pl.when(sends)
@@ -467,17 +468,28 @@
         def _():
             h_copies[o].wait_send()
     for colour, values in ((0, vr), (1, vk2)):
+        def wait_for(part, q):
+            remote(
+                values.at[HALO, v_rows], e_out.at[part, q, colour],
+                e_send.at[part, colour, 0], e_recv.at[part, colour, q], g, q,
+            ).wait_recv()
+
+        for j in range(1, MEM):
+            q = lax.rem(m + MEM - j, MEM)
+            wait_for(0, q)
+            copy = remote(
+                e_out.at[0, q, colour], e_out.at[1, q, colour],
+                fwd_send.at[colour, j], e_recv.at[1, colour, q], g, m - odd,
+            )
+            sends = jnp.logical_and(odd == 1, q // blocks != m // blocks)
+            e_copies.append((copy, sends))
+
+            @pl.when(sends)
+            def _():
+                copy.start()
+
+    for colour, values in ((0, vr), (1, vk2)):
         for q in range(MEM):
-            def wait_for(part):
-                remote(
-                    values.at[HALO, v_rows], e_out.at[part, q, colour],
-                    e_send.at[part, colour, 0], e_recv.at[part, colour, q], g, q,
-                ).wait_recv()
-
-            @pl.when(m != q)
-            def _():
-                wait_for(0)
-
             last = m == MEM - 1
             arrives = jnp.logical_or(
                 jnp.logical_and(jnp.logical_not(last), m != q), jnp.logical_and(last, g < groups - 1)
@@ -485,7 +497,10 @@
 
             @pl.when(arrives)
             def _():
-                wait_for(1)
+                remote(
+                    values.at[HALO, v_rows], e_out.at[1, q, colour],
+                    e_send.at[1, colour, 0], e_recv.at[1, colour, q], g, q,
+                ).wait_recv()
     for copy, sends in e_copies:
         if sends is None:
             copy.wait_send()
@@ -537,6 +552,7 @@
             dma((8,)),
             dma((2, 2, MEM)),
             dma((2, 2, MEM)),
+            dma((2, MEM)),
         ],
         compiler_params=pltpu.CompilerParams(collective_id=0, has_side_effects=True),
         name="smooth",

time: 45.2 us -> 44.5 us (0.985)
  Pallas kernels: 43.9 us -> 43.1 us
    pallas_call x1, Pallas kernels: 41.9 us -> 41.1 us  [smooth(): pl.pallas_call(smooth_kernel, out_shape=(pltpu.VMEM((2, MEM, 2, ROWS, 128...]
where the time goes in v7:
time: 44.5 us; the launch traced here: 43.7 us
  Pallas kernels  43.1 us (97%)
  between operations  0.64 us (1%)
    pallas_call x1, Pallas kernels, smooth(): pl.pallas_call(smooth_kernel, out_shape=(pltpu.VMEM((2, MEM, 2, ROWS, 128...  41.1 us
    pallas_call x1, Pallas kernels, prolong(): pl.pallas_call(prolong_kernel, out_shape=(jax.ShapeDtypeStruct((2, NF, NF...  2.01 us

profile of v7, /device:TPU:129, one launch (start us, length us, event | category | flops | bytes accessed | tf_op | source)
XLA Modules:
  0.0 43.7 jit_solution(9951028748229130454)
XLA Ops:
  0.6 41.1 %smooth.1 = (f32[2,8,2,32,128]{4,3,2,1,0:T(8,128)S(1)}, f32[2,4,528,128]{3,2,1,0:T(8,128)S(1)}, bf16[256,512]{1,0:T(8,128)(2,1)S(1)}, bf16[256,256]{1,0:T(8,128)(2,1)S(1)}) custom-call(f32[2,512,512]{2,1,0:T(8,128)} %p_hbm.1, f32[2,512,512]{2,1,0:T(8,128)} %s_hbm.1, f32[1,4,256]{2,1,0:T(4,128)} %side.1, f32[2,256,256]{2,1,0:T(8,128)} %end_hbm.1), custom_call_target="tpu_custom_call" | custom-call | tf_op jit(solution)/shard_map/smooth/pallas_call | solution.py:516
  41.7 2.0 %prolong.1 = (f32[2,512,512]{2,1,0:T(8,128)}, f32[1,256,256]{2,1,0:T(8,128)}) custom-call(f32[2,8,2,32,128]{4,3,2,1,0:T(8,128)S(1)} %get-tuple-element.6.e, f32[2,4,528,128]{3,2,1,0:T(8,128)S(1)} %get-tuple-element.7.p, bf16[256,512]{1,0:T(8,128)(2,1)S(1)} %get-tuple-element.8.w_fine, bf16[256,256]{1,0:T(8,128)(2,1)S(1)} %get-tuple-element.9.w_plain), custom_call_target="tpu_custom_call" | custom-call | tf_op jit(solution)/shard_map/prolong/pallas_call | solution.py:615

commit v8 on v7

--- a/solution.py
+++ b/solution.py
@@ -622,7 +622,7 @@
         out_specs=(anyspace, anyspace),
         scratch_shapes=[
             pltpu.VMEM((2, 4, CROWS + 8, 128), F32),
-            pltpu.VMEM((2, 4, NF, 128), F32),
+            pltpu.VMEM((2, 4, NF + 16, 128), F32),
             pltpu.VMEM((NC, NC), F32),
             pltpu.SemaphoreType.DMA((CHUNKS, 2, 4)),
             pltpu.SemaphoreType.DMA((CHUNKS,)),

time: 44.5 us -> 44.5 us (level)
  no operation moved by 1% of the time
where the time goes in v8:
time: 44.5 us; the launch traced here: 43.7 us
  Pallas kernels  43.1 us (97%)
  between operations  0.64 us (1%)
    pallas_call x1, Pallas kernels, smooth(): pl.pallas_call(smooth_kernel, out_shape=(pltpu.VMEM((2, MEM, 2, ROWS, 128...  41.1 us
    pallas_call x1, Pallas kernels, prolong(): pl.pallas_call(prolong_kernel, out_shape=(jax.ShapeDtypeStruct((2, NF, NF...  2.01 us

profile of v8, /device:TPU:129, one launch (start us, length us, event | category | flops | bytes accessed | tf_op | source)
XLA Modules:
  0.0 43.7 jit_solution(16683131284234300949)
XLA Ops:
  0.6 41.1 %smooth.1 = (f32[2,8,2,32,128]{4,3,2,1,0:T(8,128)S(1)}, f32[2,4,528,128]{3,2,1,0:T(8,128)S(1)}, bf16[256,512]{1,0:T(8,128)(2,1)S(1)}, bf16[256,256]{1,0:T(8,128)(2,1)S(1)}) custom-call(f32[2,512,512]{2,1,0:T(8,128)} %p_hbm.1, f32[2,512,512]{2,1,0:T(8,128)} %s_hbm.1, f32[1,4,256]{2,1,0:T(4,128)} %side.1, f32[2,256,256]{2,1,0:T(8,128)} %end_hbm.1), custom_call_target="tpu_custom_call" | custom-call | tf_op jit(solution)/shard_map/smooth/pallas_call | solution.py:516
  41.7 2.0 %prolong.1 = (f32[2,512,512]{2,1,0:T(8,128)}, f32[1,256,256]{2,1,0:T(8,128)}) custom-call(f32[2,8,2,32,128]{4,3,2,1,0:T(8,128)S(1)} %get-tuple-element.6.e, f32[2,4,528,128]{3,2,1,0:T(8,128)S(1)} %get-tuple-element.7.p, bf16[256,512]{1,0:T(8,128)(2,1)S(1)} %get-tuple-element.8.w_fine, bf16[256,256]{1,0:T(8,128)(2,1)S(1)} %get-tuple-element.9.w_plain), custom_call_target="tpu_custom_call" | custom-call | tf_op jit(solution)/shard_map/prolong/pallas_call | solution.py:615
